TPU v7x, 512 devices: a whole 4x8x8 slice. The times are simulated.
512 devices in a mesh: gy: 8 (over x, core), gx: 64 (over z, y).
Axes of the slice: x: 4, y: 8, z: 8, core: 2. Of those that a mesh axis runs over, the one named last changes fastest.
Arguments:
- position: float32 [16, 512, 128, 3], P('gy', 'gx'), may hold values from 0 to 1
- velocity: float32 [16, 512, 128, 3], P('gy', 'gx'), may hold values from -6 to 6
- particle_mass: float32 [16, 512, 128], P('gy', 'gx'), may hold values from 0.006 to 0.025
- cell_counts: int32 [16, 512], P('gy', 'gx'), may hold values from 64 to 128
- shear_shift: int32 [1], replicated, may hold values from 252 to 260
Outputs:
- density: float32 [16, 512, 128], P('gy', 'gx')
- acceleration: float32 [16, 512, 128, 3], P('gy', 'gx')
Inputs may be any that keep to these rules, and one draw needn't show every extreme that they name: `shear_shift`: the offset is a whole number of cells from 252 to 260.
All inputs are finite; a program needn't handle non-finite values.
Results may differ from a plain program's by a relative error of at most 0.0003.
Values sent between devices are 32-bit elements; how exact they have to be, the bound alone decides.
No kernel may reach another device: no remote copies, remote signals or barrier semaphores. Data moves between devices by JAX's collectives and lax.ppermute only.
A program may use at most 64 MiB of HBM per device.

v0:
```python
import math

import jax
import jax.numpy as jnp
from jax import lax
from jax.sharding import PartitionSpec as P

SMOOTHING = 0.5
KERNEL_NORM = 1.0 / (math.pi * SMOOTHING**3)
SOUND_SQ = 0.2
VISCOSITY = 0.05
SOFTENING = 0.0025
SHEAR_JUMP = 1.0


def with_halo(x, sides, width):
    for axis, dim in sides:
        peers, length = (lax.axis_size(axis), x.shape[dim])
        up = [(i, (i + 1) % peers) for i in range(peers)]
        down = [(j, i) for i, j in up]
        last = lax.slice_in_dim(x, length - width, length, axis=dim)
        first = lax.slice_in_dim(x, 0, width, axis=dim)
        before = lax.ppermute(last, axis, up)
        after = lax.ppermute(first, axis, down)
        x = jnp.concatenate([before, x, after], axis=dim)
    return x


def passed_along(x, axis, by):
    peers = lax.axis_size(axis)
    return lax.ppermute(x, axis, [(i, (i + by) % peers) for i in range(peers)])


def kernel_value(dist_sq):
    distance = jnp.sqrt(dist_sq)
    ratio = distance / SMOOTHING
    inner_part = 1.0 - 1.5 * ratio * ratio + 0.75 * ratio * ratio * ratio
    outer_part = 0.25 * jnp.maximum(2.0 - ratio, 0.0) ** 3
    return KERNEL_NORM * jnp.where(ratio < 1.0, inner_part, outer_part)


def kernel_slope(dist_sq):
    distance = jnp.sqrt(dist_sq)
    ratio = distance / SMOOTHING
    inner_part = (-3.0 + 2.25 * ratio) / (SMOOTHING * SMOOTHING)
    outer_part = (
        -0.75 * jnp.maximum(2.0 - ratio, 0.0) ** 2 / (SMOOTHING * jnp.maximum(distance, SMOOTHING))
    )
    return KERNEL_NORM * jnp.where(ratio < 1.0, inner_part, outer_part)


def stencil(padded, row_index):
    band = lax.dynamic_slice_in_dim(padded, row_index, 3, 0)
    columns = padded.shape[1] - 2
    cell_parts = []
    for up_down in range(3):
        for across in range(3):
            cell_parts.append(band[up_down, across : across + columns])
    return jnp.concatenate(cell_parts, axis=2)


def stencil_offsets(slots, dtype):
    parts = []
    for up_down in range(3):
        for across in range(3):
            entry = jnp.array([across - 1.0, up_down - 1.0, 0.0], dtype)
            parts.append(jnp.broadcast_to(entry[:, None], (3, slots)))
    return jnp.concatenate(parts, axis=1)


def own_cells(padded, row_index):
    return lax.dynamic_slice_in_dim(padded, row_index + 1, 1, 0)[0, 1:-1]


def pair_offsets(own_part, near_cells):
    shift_table = stencil_offsets(own_part.shape[2], near_cells.dtype)
    near_pos = near_cells[:, 0:3, :] + shift_table[None]
    return own_part[:, 0:3, :, None] - near_pos[:, :, None, :]


def densities(padded):

    def densities_one_row(row_index):
        near_cells = stencil(padded, row_index)
        own_part = own_cells(padded, row_index)
        offsets = pair_offsets(own_part, near_cells)
        dist_sq = jnp.sum(offsets * offsets, axis=1)
        return jnp.sum(near_cells[:, 6][:, None, :] * kernel_value(dist_sq), axis=-1)

    return lax.map(densities_one_row, jnp.arange(padded.shape[0] - 2, dtype=jnp.int32))


def forces(padded, rho_pad):
    rho_cells = rho_pad[:, :, None, :]

    def forces_one_row(row_index):
        near_cells = stencil(padded, row_index)
        near_rho = stencil(rho_cells, row_index)[:, 0][:, None, :]
        own_part = own_cells(padded, row_index)
        own_rho = own_cells(rho_cells, row_index)[:, 0][:, :, None]
        offsets = pair_offsets(own_part, near_cells)
        dist_sq = jnp.sum(offsets * offsets, axis=1)
        slope = kernel_slope(dist_sq)
        near_mass = near_cells[:, 6][:, None, :]
        pressure_term = -(SOUND_SQ / own_rho + SOUND_SQ / near_rho) * near_mass * slope
        viscous_term = (
            2.0
            * VISCOSITY
            * near_mass
            * slope
            * dist_sq
            / ((dist_sq + SOFTENING) * own_rho * near_rho)
        )
        relative = own_part[:, 3:6, :, None] - near_cells[:, 3:6, None, :]
        return jnp.sum(pressure_term[:, None] * offsets + viscous_term[:, None] * relative, axis=-1)

    return lax.map(forces_one_row, jnp.arange(padded.shape[0] - 2, dtype=jnp.int32))


def ghost_block(fields, ghost_width, shift_cells, vx_jump):
    columns = fields.shape[1]
    padded_y = with_halo(fields, (("gy", 0),), ghost_width)
    slab_index = lax.axis_index("gy")
    last_slab = lax.axis_size("gy") - 1
    total_columns = columns * lax.axis_size("gx")
    column_start = lax.axis_index("gx") * columns - ghost_width
    window = columns + 2 * ghost_width
    edge_rows = jnp.concatenate([padded_y[:ghost_width], padded_y[-ghost_width:]], axis=0)
    padded_xy = with_halo(padded_y, (("gx", 1),), ghost_width)
    half_cycle = lax.axis_size("gx") // 2
    far_parts = []
    for step in range(3):
        far_parts.append(passed_along(edge_rows, "gx", -(half_cycle - 1 + step)))
    near_rows = jnp.concatenate(far_parts, axis=1)
    base_column = (lax.axis_index("gx") + half_cycle - 1) * columns
    lower_start = (column_start + shift_cells - base_column) % total_columns
    upper_start = (column_start - shift_cells - base_column) % total_columns
    lower_far = lax.dynamic_slice_in_dim(near_rows[:ghost_width], lower_start, window, 1)
    upper_far = lax.dynamic_slice_in_dim(near_rows[ghost_width:], upper_start, window, 1)
    lower_rows = jnp.where(slab_index == 0, lower_far - vx_jump, padded_xy[:ghost_width])
    upper_rows = jnp.where(slab_index == last_slab, upper_far + vx_jump, padded_xy[-ghost_width:])
    return jnp.concatenate([lower_rows, padded_xy[ghost_width:-ghost_width], upper_rows], axis=0)


def local(position, velocity, particle_mass, cell_counts, shear_shift):
    shift_cells = shear_shift[0]
    slots = position.shape[2]
    is_valid = jnp.arange(slots, dtype=jnp.int32)[None, None, :] < cell_counts[:, :, None]
    weight = jnp.where(is_valid, particle_mass, 0.0)
    fields = jnp.concatenate(
        [
            jnp.transpose(position, (0, 1, 3, 2)),
            jnp.transpose(velocity, (0, 1, 3, 2)),
            weight[:, :, None, :],
        ],
        axis=2,
    )
    vx_jump = jnp.array([0.0, 0.0, 0.0, SHEAR_JUMP, 0.0, 0.0, 0.0], fields.dtype)[:, None]
    padded_two = ghost_block(fields, 2, shift_cells, vx_jump)
    cycle_rho = densities(padded_two)
    cycle_weight = padded_two[1:-1, 1:-1, 6, :]
    rho_pad = jnp.where(cycle_weight > 0.0, cycle_rho, 1.0)
    padded_one = padded_two[1:-1, 1:-1]
    density_raw = cycle_rho[1:-1, 1:-1]
    accel = jnp.transpose(forces(padded_one, rho_pad), (0, 1, 3, 2))
    density = jnp.where(is_valid, density_raw, 0.0)
    acceleration = jnp.where(is_valid[..., None], accel, 0.0)
    return (density, acceleration)


def solution(mesh):
    placed = (
        P("gy", "gx", None, None),
        P("gy", "gx", None, None),
        P("gy", "gx", None),
        P("gy", "gx"),
        P(),
    )
    return jax.shard_map(
        local,
        mesh=mesh,
        in_specs=placed,
        out_specs=(P("gy", "gx", None), P("gy", "gx", None, None)),
        check_vma=False,
    )
```

profile of v0, /device:TPU:191, one launch (start us, length us, event | category | flops | bytes accessed | tf_op | source)
XLA Modules:
  0.0 134.0 jit_solution(8340520923289944420)
XLA Ops:
  4.5 3.3 %collective-permute-done.1 = f32[2,8,7,128]{3,1,2,0:T(8,128)S(1)} collective-permute-done((f32[2,8,7,128]{3,1,2,0:T(8,128)S(1)}, f32[2,8,7,128]{3,1,2,0:T(8,128)S(1)}, u32[]{:S(2)}, u32[]{:S(2)}) %collective-permute-start.1) | collective-permute-done | bytes 57376 | tf_op jit(solution)/shard_map/ppermute | solution.py:24
  7.9 0.8 pad_maximum_fusion.7
  8.7 3.2 %collective-permute-start.5 = (f32[6,2,7,128]{3,1,2,0:T(2,128)S(1)}, f32[6,2,7,128]{3,1,2,0:T(2,128)S(1)}, u32[]{:S(2)}, u32[]{:S(2)}) collective-permute-start(f32[6,2,7,128]{3,1,2,0:T(2,128)S(1)} %get-tuple-element.455), channel_id=1, source_target_pairs={{0,1},{1,2},{2,3},{3,4},{4,5},{5,6},{6,7},{7,8},{8,9},{9,10},{10,1... | collective-permute-start | bytes 129032 | tf_op jit(solution)/shard_map/ppermute | solution.py:23
  11.9 2.1 %collective-permute-start.6 = (f32[6,2,7,128]{3,1,2,0:T(2,128)S(1)}, f32[6,2,7,128]{3,1,2,0:T(2,128)S(1)}, u32[]{:S(2)}, u32[]{:S(2)}) collective-permute-start(f32[6,2,7,128]{3,1,2,0:T(2,128)S(1)} %get-tuple-element.456), channel_id=1, source_target_pairs={{1,0},{2,1},{3,2},{4,3},{5,4},{6,5},{7,6},{8,7},{9,8},{10,9},{11,1... | collective-permute-start | bytes 129032 | tf_op jit(solution)/shard_map/ppermute | solution.py:24
  14.0 10.2 %collective-permute-start.2 = (f32[4,8,7,128]{3,1,2,0:T(8,128)S(1)}, f32[4,8,7,128]{3,1,2,0:T(8,128)S(1)}, u32[]{:S(2)}, u32[]{:S(2)}) collective-permute-start(f32[4,8,7,128]{3,1,2,0:T(8,128)S(1)} %constant_dynamic-update-slice_fusion.45), channel_id=1, source_target_pairs={{0,33},{1,34},{2,35},{3,36},{4,37},{5,38},{6,39},{7,40},{8,41},{9,... | collective-permute-start | bytes 344072 | tf_op jit(solution)/shard_map/ppermute | solution.py:31
  24.2 1.9 %collective-permute-start.3 = (f32[4,8,7,128]{3,1,2,0:T(8,128)S(1)}, f32[4,8,7,128]{3,1,2,0:T(8,128)S(1)}, u32[]{:S(2)}, u32[]{:S(2)}) collective-permute-start(f32[4,8,7,128]{3,1,2,0:T(8,128)S(1)} %constant_dynamic-update-slice_fusion.45), channel_id=1, source_target_pairs={{0,32},{1,33},{2,34},{3,35},{4,36},{5,37},{6,38},{7,39},{8,40},{9,... | collective-permute-start | bytes 344072 | tf_op jit(solution)/shard_map/ppermute | solution.py:31
  26.1 6.8 %collective-permute-start.4 = (f32[4,8,7,128]{3,1,2,0:T(8,128)S(1)}, f32[4,8,7,128]{3,1,2,0:T(8,128)S(1)}, u32[]{:S(2)}, u32[]{:S(2)}) collective-permute-start(f32[4,8,7,128]{3,1,2,0:T(8,128)S(1)} %constant_dynamic-update-slice_fusion.45), channel_id=1, source_target_pairs={{0,31},{1,32},{2,33},{3,34},{4,35},{5,36},{6,37},{7,38},{8,39},{9,... | collective-permute-start | bytes 344072 | tf_op jit(solution)/shard_map/ppermute | solution.py:31
  33.9 18.9 %collective-permute-done.3 = f32[4,8,7,128]{3,1,2,0:T(8,128)S(1)} collective-permute-done((f32[4,8,7,128]{3,1,2,0:T(8,128)S(1)}, f32[4,8,7,128]{3,1,2,0:T(8,128)S(1)}, u32[]{:S(2)}, u32[]{:S(2)}) %collective-permute-start.3) | collective-permute-done | bytes 114720 | tf_op jit(solution)/shard_map/ppermute | solution.py:31
  53.8 47.0 %while.28 = (s32[]{:T(128)}, f32[4,10,128]{2,1,0:T(8,128)S(1)}, s32[4]{0:T(128)S(1)}, f32[6,12,7,128]{3,1,2,0:T(8,128)S(1)}, f32[3]{0:T(128)S(1)}, /*index=5*/f3...) while((s32[]{:T(128)}, f32[4,10,128]{2,1,0:T(8,128)S(1)}, ...), condition=%wide.region_3.4_spmd.clone.clone, body=%wide.region_0.3_spmd.sunk.clone.sunk.clone | while | flops 36908812 | bytes 13842773 | solution.py:90
  58.6 2.2 %multiply_reduce_fusion.3 = f32[10,128,1152]{2,1,0:T(8,128)S(1)} fusion(f32[10,3,1152]{2,1,0:T(4,128)S(1)} %copy.88, f32[10,3,128]{2,1,0:T(4,128)S(1)} %copy.89), kind=kLoop, calls=%fused_computation.clone.1.clone | loop fusion | flops 11796480 | bytes 6051840 | tf_op jit(solution)/shard_map/while/body/eval_jaxpr/reduce_sum | solution.py:87
  60.8 4.7 %fusion.61 = f32[10,128]{1,0:T(8,128)S(1)} fusion(f32[10,128,1152]{2,1,0:T(8,128)S(1)} %multiply_reduce_fusion.3, f32[10,1152]{1,0:T(8,128)S(1)} %fusion.60), kind=kLoop, calls=%fused_computation.6.clone.1.clone | loop fusion | flops 25066240 | bytes 5949440 | tf_op jit(solution)/shard_map/while/body/eval_jaxpr/reduce_sum | solution.py:88
  70.3 2.2 %multiply_reduce_fusion.3 = f32[10,128,1152]{2,1,0:T(8,128)S(1)} fusion(f32[10,3,1152]{2,1,0:T(4,128)S(1)} %copy.88, f32[10,3,128]{2,1,0:T(4,128)S(1)} %copy.89), kind=kLoop, calls=%fused_computation.clone.1.clone | loop fusion | flops 11796480 | bytes 6051840 | tf_op jit(solution)/shard_map/while/body/eval_jaxpr/reduce_sum | solution.py:87
  72.6 4.7 %fusion.61 = f32[10,128]{1,0:T(8,128)S(1)} fusion(f32[10,128,1152]{2,1,0:T(8,128)S(1)} %multiply_reduce_fusion.3, f32[10,1152]{1,0:T(8,128)S(1)} %fusion.60), kind=kLoop, calls=%fused_computation.6.clone.1.clone | loop fusion | flops 25066240 | bytes 5949440 | tf_op jit(solution)/shard_map/while/body/eval_jaxpr/reduce_sum | solution.py:88
  82.1 2.2 %multiply_reduce_fusion.3 = f32[10,128,1152]{2,1,0:T(8,128)S(1)} fusion(f32[10,3,1152]{2,1,0:T(4,128)S(1)} %copy.88, f32[10,3,128]{2,1,0:T(4,128)S(1)} %copy.89), kind=kLoop, calls=%fused_computation.clone.1.clone | loop fusion | flops 11796480 | bytes 6051840 | tf_op jit(solution)/shard_map/while/body/eval_jaxpr/reduce_sum | solution.py:87
  84.3 4.7 %fusion.61 = f32[10,128]{1,0:T(8,128)S(1)} fusion(f32[10,128,1152]{2,1,0:T(8,128)S(1)} %multiply_reduce_fusion.3, f32[10,1152]{1,0:T(8,128)S(1)} %fusion.60), kind=kLoop, calls=%fused_computation.6.clone.1.clone | loop fusion | flops 25066240 | bytes 5949440 | tf_op jit(solution)/shard_map/while/body/eval_jaxpr/reduce_sum | solution.py:88
  93.8 2.2 %multiply_reduce_fusion.3 = f32[10,128,1152]{2,1,0:T(8,128)S(1)} fusion(f32[10,3,1152]{2,1,0:T(4,128)S(1)} %copy.88, f32[10,3,128]{2,1,0:T(4,128)S(1)} %copy.89), kind=kLoop, calls=%fused_computation.clone.1.clone | loop fusion | flops 11796480 | bytes 6051840 | tf_op jit(solution)/shard_map/while/body/eval_jaxpr/reduce_sum | solution.py:87
  96.1 4.7 %fusion.61 = f32[10,128]{1,0:T(8,128)S(1)} fusion(f32[10,128,1152]{2,1,0:T(8,128)S(1)} %multiply_reduce_fusion.3, f32[10,1152]{1,0:T(8,128)S(1)} %fusion.60), kind=kLoop, calls=%fused_computation.6.clone.1.clone | loop fusion | flops 25066240 | bytes 5949440 | tf_op jit(solution)/shard_map/while/body/eval_jaxpr/reduce_sum | solution.py:88
  101.6 31.8 %while.29 = (s32[]{:T(128)}, f32[2,8,3,128]{3,1,2,0:T(8,128)S(1)}, s32[2]{0:T(128)S(1)}, f32[4,10,1,128]{3,1,2,0:T(8,128)S(1)}, f32[4,10,7,128]{3,1,2,0:T(8,128)...) while((s32[]{:T(128)}, f32[2,8,3,128]{3,1,2,0:T(8,128)S(1)}, ...), condition=%wide.region_7.8_spmd.clone.clone, body=%wide.region_4.7_spmd.sunk.clone.sunk.clone | while | flops 59026444 | bytes 30813660 | solution.py:117
  106.3 1.7 %fusion.63 = f32[8,128,1152]{2,1,0:T(8,128)S(1)} fusion(f32[8,3,1152]{2,1,0:T(4,128)S(1)} %copy.93, f32[8,3,128]{2,1,0:T(4,128)S(1)} %copy.94), kind=kLoop, calls=%fused_computation.43.clone.1.clone | loop fusion | flops 9437184 | bytes 4841472 | tf_op jit(solution)/shard_map/while/body/eval_jaxpr/reduce_sum | solution.py:102
  108.4 5.2 %multiply_multiply_fusion.5 = (f32[8,128,1152]{2,1,0:T(8,128)S(1)}, f32[8,128,1152]{2,1,0:T(8,128)S(1)}) fusion(f32[8,1152]{1,0:T(8,128)S(1)} %get-tuple-element.590, f32[8,1152]{1,0:T(8,128)S(1)} %broadcast_divide_fusion.7, f32[8,128]{1,0:T(8,128)S(1)} %get-tuple-element.592, f32[8,128,1152]{2,1,0:T(8,128)S(1)} %fusion.63, ...), kind=kLoop, calls=%fused_computation.47.clone.1.clone | loop fusion | flops 28311552 | bytes 14311424 | tf_op jit(solution)/shard_map/while/body/eval_jaxpr/mul | solution.py:105
  113.6 3.8 %fusion.64 = f32[8,3,128]{2,1,0:T(4,128)S(1)} fusion(f32[8,3,1152]{2,1,0:T(4,128)S(1)} %copy.91, f32[8,3,128]{2,1,0:T(4,128)S(1)} %copy.92, f32[8,128,1152]{2,1,0:T(8,128)S(1)} %get-tuple-element.597, f32[8,128,1152]{2,1,0:T(8,128)S(1)} %get-tuple-element.598, f32[8,3,1152]{2,1,0:T(4,128)S(1)} %copy.93, f32[8,3,128]{2,1,0:T(4,128)S(1)} %copy.94), kind=kLoop, calls=%fused_computation.45.clone.1.clone | loop fusion | flops 21230592 | bytes 9695232 | tf_op jit(solution)/shard_map/while/body/eval_jaxpr/reduce_sum | solution.py:115
  122.2 1.7 %fusion.63 = f32[8,128,1152]{2,1,0:T(8,128)S(1)} fusion(f32[8,3,1152]{2,1,0:T(4,128)S(1)} %copy.93, f32[8,3,128]{2,1,0:T(4,128)S(1)} %copy.94), kind=kLoop, calls=%fused_computation.43.clone.1.clone | loop fusion | flops 9437184 | bytes 4841472 | tf_op jit(solution)/shard_map/while/body/eval_jaxpr/reduce_sum | solution.py:102
  124.3 5.2 %multiply_multiply_fusion.5 = (f32[8,128,1152]{2,1,0:T(8,128)S(1)}, f32[8,128,1152]{2,1,0:T(8,128)S(1)}) fusion(f32[8,1152]{1,0:T(8,128)S(1)} %get-tuple-element.590, f32[8,1152]{1,0:T(8,128)S(1)} %broadcast_divide_fusion.7, f32[8,128]{1,0:T(8,128)S(1)} %get-tuple-element.592, f32[8,128,1152]{2,1,0:T(8,128)S(1)} %fusion.63, ...), kind=kLoop, calls=%fused_computation.47.clone.1.clone | loop fusion | flops 28311552 | bytes 14311424 | tf_op jit(solution)/shard_map/while/body/eval_jaxpr/mul | solution.py:105
  129.5 3.8 %fusion.64 = f32[8,3,128]{2,1,0:T(4,128)S(1)} fusion(f32[8,3,1152]{2,1,0:T(4,128)S(1)} %copy.91, f32[8,3,128]{2,1,0:T(4,128)S(1)} %copy.92, f32[8,128,1152]{2,1,0:T(8,128)S(1)} %get-tuple-element.597, f32[8,128,1152]{2,1,0:T(8,128)S(1)} %get-tuple-element.598, f32[8,3,1152]{2,1,0:T(4,128)S(1)} %copy.93, f32[8,3,128]{2,1,0:T(4,128)S(1)} %copy.94), kind=kLoop, calls=%fused_computation.45.clone.1.clone | loop fusion | flops 21230592 | bytes 9695232 | tf_op jit(solution)/shard_map/while/body/eval_jaxpr/reduce_sum | solution.py:115
  (245 shorter events, 15.7 us)
Async XLA Ops:
  0.6 53.1 %copy-start = (f32[3]{0:T(128)S(1)}, f32[3]{0:T(128)}, u32[]{:S(2)}) copy-start(f32[3]{0:T(128)} %constant.227.clone..sunk.4) | copy-start | bytes 40
  0.6 53.1 %copy-start.1 = (f32[3]{0:T(128)S(1)}, f32[3]{0:T(128)}, u32[]{:S(2)}) copy-start(f32[3]{0:T(128)} %constant.228.clone..sunk.4) | copy-start | bytes 40
  0.7 53.1 %copy-start.2 = (f32[3]{0:T(128)S(1)}, f32[3]{0:T(128)}, u32[]{:S(2)}) copy-start(f32[3]{0:T(128)} %constant.229.clone..sunk.4) | copy-start | bytes 40
  0.7 53.1 %copy-start.3 = (f32[3]{0:T(128)S(1)}, f32[3]{0:T(128)}, u32[]{:S(2)}) copy-start(f32[3]{0:T(128)} %constant.230.clone..sunk.4) | copy-start | bytes 40
  0.7 53.1 %copy-start.4 = (f32[3]{0:T(128)S(1)}, f32[3]{0:T(128)}, u32[]{:S(2)}) copy-start(f32[3]{0:T(128)} %constant.232.clone..sunk.4) | copy-start | bytes 40
  0.7 53.1 %copy-start.5 = (f32[3]{0:T(128)S(1)}, f32[3]{0:T(128)}, u32[]{:S(2)}) copy-start(f32[3]{0:T(128)} %constant.233.clone..sunk.4) | copy-start | bytes 40
  0.7 53.1 %copy-start.6 = (f32[3]{0:T(128)S(1)}, f32[3]{0:T(128)}, u32[]{:S(2)}) copy-start(f32[3]{0:T(128)} %constant.234.clone..sunk.4) | copy-start | bytes 40
  0.7 53.1 %copy-start.7 = (f32[3]{0:T(128)S(1)}, f32[3]{0:T(128)}, u32[]{:S(2)}) copy-start(f32[3]{0:T(128)} %constant.235.clone..sunk.4) | copy-start | bytes 40
  2.3 2.2 %collective-permute-start = (f32[2,8,7,128]{3,1,2,0:T(8,128)S(1)}, f32[2,8,7,128]{3,1,2,0:T(8,128)S(1)}, u32[]{:S(2)}, u32[]{:S(2)}) collective-permute-start(f32[2,8,7,128]{3,1,2,0:T(8,128)S(1)} %pad_maximum_fusion.2), channel_id=1, source_target_pairs={{0,64},{64,128},{128,192},{192,256},{256,320},{320,384},{384,448},... | collective-permute-start | bytes 172040 | tf_op jit(solution)/shard_map/ppermute | solution.py:23
  3.0 4.8 %collective-permute-start.1 = (f32[2,8,7,128]{3,1,2,0:T(8,128)S(1)}, f32[2,8,7,128]{3,1,2,0:T(8,128)S(1)}, u32[]{:S(2)}, u32[]{:S(2)}) collective-permute-start(f32[2,8,7,128]{3,1,2,0:T(8,128)S(1)} %pad_maximum_fusion.2), channel_id=1, source_target_pairs={{64,0},{128,64},{192,128},{256,192},{320,256},{384,320},{448,384},... | collective-permute-start | bytes 172040 | tf_op jit(solution)/shard_map/ppermute | solution.py:24
  8.7 24.3 %collective-permute-start.5 = (f32[6,2,7,128]{3,1,2,0:T(2,128)S(1)}, f32[6,2,7,128]{3,1,2,0:T(2,128)S(1)}, u32[]{:S(2)}, u32[]{:S(2)}) collective-permute-start(f32[6,2,7,128]{3,1,2,0:T(2,128)S(1)} %get-tuple-element.455), channel_id=1, source_target_pairs={{0,1},{1,2},{2,3},{3,4},{4,5},{5,6},{6,7},{7,8},{8,9},{9,10},{10,1... | collective-permute-start | bytes 129032 | tf_op jit(solution)/shard_map/ppermute | solution.py:23
  11.9 21.1 %collective-permute-start.6 = (f32[6,2,7,128]{3,1,2,0:T(2,128)S(1)}, f32[6,2,7,128]{3,1,2,0:T(2,128)S(1)}, u32[]{:S(2)}, u32[]{:S(2)}) collective-permute-start(f32[6,2,7,128]{3,1,2,0:T(2,128)S(1)} %get-tuple-element.456), channel_id=1, source_target_pairs={{1,0},{2,1},{3,2},{4,3},{5,4},{6,5},{7,6},{8,7},{9,8},{10,9},{11,1... | collective-permute-start | bytes 129032 | tf_op jit(solution)/shard_map/ppermute | solution.py:24
  14.0 19.8 %collective-permute-start.2 = (f32[4,8,7,128]{3,1,2,0:T(8,128)S(1)}, f32[4,8,7,128]{3,1,2,0:T(8,128)S(1)}, u32[]{:S(2)}, u32[]{:S(2)}) collective-permute-start(f32[4,8,7,128]{3,1,2,0:T(8,128)S(1)} %constant_dynamic-update-slice_fusion.45), channel_id=1, source_target_pairs={{0,33},{1,34},{2,35},{3,36},{4,37},{5,38},{6,39},{7,40},{8,41},{9,... | collective-permute-start | bytes 344072 | tf_op jit(solution)/shard_map/ppermute | solution.py:31
  24.2 28.6 %collective-permute-start.3 = (f32[4,8,7,128]{3,1,2,0:T(8,128)S(1)}, f32[4,8,7,128]{3,1,2,0:T(8,128)S(1)}, u32[]{:S(2)}, u32[]{:S(2)}) collective-permute-start(f32[4,8,7,128]{3,1,2,0:T(8,128)S(1)} %constant_dynamic-update-slice_fusion.45), channel_id=1, source_target_pairs={{0,32},{1,33},{2,34},{3,35},{4,36},{5,37},{6,38},{7,39},{8,40},{9,... | collective-permute-start | bytes 344072 | tf_op jit(solution)/shard_map/ppermute | solution.py:31
  26.1 26.7 %collective-permute-start.4 = (f32[4,8,7,128]{3,1,2,0:T(8,128)S(1)}, f32[4,8,7,128]{3,1,2,0:T(8,128)S(1)}, u32[]{:S(2)}, u32[]{:S(2)}) collective-permute-start(f32[4,8,7,128]{3,1,2,0:T(8,128)S(1)} %constant_dynamic-update-slice_fusion.45), channel_id=1, source_target_pairs={{0,31},{1,32},{2,33},{3,34},{4,35},{5,36},{6,37},{7,38},{8,39},{9,... | collective-permute-start | bytes 344072 | tf_op jit(solution)/shard_map/ppermute | solution.py:31
  53.8 47.0 %copy-start.8 = (s32[2,8]{1,0:T(2,128)S(1)}, s32[2,8]{1,0:T(2,128)}, u32[]{:S(2)}) copy-start(s32[2,8]{1,0:T(2,128)} %param.31) | copy-start | bytes 196
where the time goes:
time: 135 us; the launch traced here: 134 us
  other arithmetic  55.5 us (41%)
  starting transfers between devices  25 us (19%)
  waiting for transfers between devices  22.3 us (17%)
  loops' own time  20.2 us (15%)
  local copies, waits for them, and re-layouts  9.4 us (7%)
  between operations  1.7 us (1%)
    ppermute x3, waiting for transfers between devices, passed_along(): return lax.ppermute(x, axis, [(i, (i + by) % peers) for i in range(peers)])  18.9 us
    ppermute x3, starting transfers between devices, passed_along(): return lax.ppermute(x, axis, [(i, (i + by) % peers) for i in range(peers)])  18.9 us
    reduce_sum x4, other arithmetic, densities_one_row(): jnp.sum(near_cells[:, 6][:, None, :] * kernel_value(dist_sq), axis=-1)  18.9 us
    another operation x1, loops' own time, densities(): lax.map(densities_one_row, jnp.arange(padded.shape[0] - 2, dtype=jnp.int32))  13.3 us
    mul x4, other arithmetic, forces_one_row(): -(SOUND_SQ / own_rho + SOUND_SQ / near_rho) * near_mass * slope  10.4 us
    reduce_sum x4, other arithmetic, densities_one_row(): dist_sq = jnp.sum(offsets * offsets, axis=1)  8.8 us
    reduce_sum x2, other arithmetic, forces_one_row(): jnp.sum(pressure_term[:, None] * offsets + viscous_term[:, None] * relati...  7.69 us
    another operation x1, loops' own time, forces(): lax.map(forces_one_row, jnp.arange(padded.shape[0] - 2, dtype=jnp.int32))  6.97 us
  transfers between devices with their start and end apart: 7, of which 2 were waited for; matrix products, arithmetic and copies ran while one was open for 1% of the time, Pallas kernels for 0%

commit v1 on v0

v1 whole, which is shorter than its diff:
```python
import functools
import math

import jax
import jax.numpy as jnp
from jax import lax
from jax.experimental import pallas as pl
from jax.experimental.pallas import tpu as pltpu
from jax.sharding import PartitionSpec as P

SMOOTHING = 0.5
KERNEL_NORM = 1.0 / (math.pi * SMOOTHING**3)
SOUND_SQ = 0.2
VISCOSITY = 0.05
SOFTENING = 0.0025
SHEAR_JUMP = 1.0

ROWS, COLS, PLACES = 6, 12, 16
DEPTH = 32
NEAR, FAR = 7, 4
SENT = 136
BF16, F32 = jnp.bfloat16, jnp.float32
NEIGHBOURS = [(a, b) for a in (-1, 0, 1) for b in (-1, 0, 1)]
VMEM = pl.BlockSpec(memory_space=pltpu.VMEM)
SMEM = pl.BlockSpec(memory_space=pltpu.SMEM)


def pack_kernel(counts, pos, vel, mass, out):
    slot = lax.broadcasted_iota(jnp.int32, (8, 128), 1)
    column = lax.broadcasted_iota(jnp.int32, (8, 128), 0)
    for row in range(2):
        limit = jnp.zeros((8, 128), jnp.int32)
        for c in range(8):
            limit = jnp.where(column == c, counts[row, c], limit)
        out[row, 0:3] = pos[row]
        out[row, 3:6] = vel[row]
        out[row, 6] = jnp.where(slot < limit, mass[row], 0.0)


def window_kernel(info, left, own, right, same_out, far_out):
    odd, start = info[0], info[1]
    for out, shift in ((same_out, 6), (far_out, start)):
        near_row = jnp.where(odd == 1, 1, 0)
        if out is same_out:
            near_row = 1 - near_row
        place = 0
        for row, fields in ((near_row, range(NEAR)), (1 - near_row, (0, 1, 2, 6))):
            for f in fields:
                wide = jnp.concatenate([left[row, f], own[row, f], right[row, f]], axis=0)
                if out is same_out:
                    piece = wide[6:18]
                else:
                    piece = pltpu.roll(wide, 24 - shift, 0)[0:COLS]
                out[place : place + COLS, :] = piece
                place += COLS
        out[place:SENT, :] = jnp.zeros((SENT - place, 128), F32)


def parts_of(x, count):
    parts = []
    for _ in range(count - 1):
        part = x.astype(BF16).astype(F32)
        parts.append(part)
        x = x - part
    parts.append(x.astype(BF16).astype(F32))
    return parts


def main_kernel(
    info, jump_ref, left, own, right, same, far, density, accel,
    fields, jrows, irows, crows, jcols, masses, scales, rhos, dist, sums,
):
    odd, jump = info[0], jump_ref[0]

    fields[...] = jnp.zeros_like(fields)
    for row in range(2):
        for f in range(7):
            fields[2 + row, f, 0:2, :] = left[row, f, 6:8, :]
            fields[2 + row, f, 2:10, :] = own[row, f]
            fields[2 + row, f, 10:12, :] = right[row, f, 0:2, :]
    same_near = jnp.where(odd == 1, 1, 4)
    far_near = 5 - same_near
    for piece, near in ((same, same_near), (far, far_near)):
        second = jnp.where(near == 1, 0, 5)
        for f in range(NEAR):
            value = piece[f * COLS : (f + 1) * COLS, :]
            if piece is far and f == 3:
                value = value + jump
            fields[near, f, 0:COLS, :] = value
        for n, f in enumerate((0, 1, 2, 6)):
            at = (NEAR + n) * COLS
            fields[second, f, 0:COLS, :] = piece[at : at + COLS, :]

    for n, (a, b) in enumerate(NEIGHBOURS):
        k = lax.broadcasted_iota(jnp.int32, (DEPTH, 128), 0)
        scale = jnp.where(k < 18, 1.0, 0.0)
        scale = jnp.where((k >= 18) & (k < 22), float(b), scale)
        scale = jnp.where((k >= 22) & (k < 26), float(a), scale)
        scale = jnp.where(k == 26, float(a * a + b * b), scale)
        scales[0, n] = scale
        scale = jnp.where((k == 4) | (k == 10) | (k == 20) | (k == 26), float(b), 1.0)
        scale = jnp.where((k == 5) | (k == 11) | (k == 21) | (k == 27), float(a), scale)
        scales[1, n] = scale

    def build(step, carry):
        row, half = step // 2, step % 2
        base = step * (8 * DEPTH)
        one = jnp.ones((8, 128), F32)
        zero = jnp.zeros((8, 128), F32)
        cells = pl.ds(pl.multiple_of(half * 8, 8), 8)

        def put(table, k, value):
            table[pl.ds(base + k, 8, stride=DEPTH), :] = value

        norm = zero
        for f in range(3):
            x = 2.0 * fields[row, f, cells, :] - 1.0
            high, low = parts_of(x, 2)
            both = high + low
            norm = norm + both * both
            for k, (mine, other) in enumerate(((high, high), (high, low), (low, high), (low, low))):
                put(jrows, 4 * f + k, mine)
                put(irows, 4 * f + k, -2.0 * other)
            if f < 2:
                at = 18 + 4 * f
                put(jrows, at, one)
                put(jrows, at + 1, one)
                put(jrows, at + 2, high)
                put(jrows, at + 3, low)
                put(irows, at, -4.0 * high)
                put(irows, at + 1, -4.0 * low)
                put(irows, at + 2, 4.0 * one)
                put(irows, at + 3, 4.0 * one)
        for k, part in enumerate(parts_of(norm, 3)):
            put(jrows, 12 + k, part)
            put(irows, 12 + k, one)
            put(jrows, 15 + k, one)
            put(irows, 15 + k, part)
        put(jrows, 26, one)
        put(irows, 26, 4.0 * one)
        for k, part in enumerate(parts_of(fields[row, 6, cells, :], 3)):
            put(jrows, 27 + k, part)
        for k in (30, 31):
            put(jrows, k, zero)
        for k in range(27, 32):
            put(irows, k, zero)
        return carry

    lax.fori_loop(0, ROWS * 2, build, 0)

    k = lax.broadcasted_iota(jnp.int32, (DEPTH, 128), 0)
    pick_mass = jnp.where((k >= 27) & (k < 30), 1.0, 0.0).astype(BF16)

    def turn(cell, carry):
        table = jrows[pl.ds(pl.multiple_of(cell * DEPTH, DEPTH), DEPTH), :]
        flipped = table.T.astype(BF16)
        jcols[cell] = flipped
        masses[cell] = jnp.dot(flipped, pick_mass, preferred_element_type=F32)
        return carry

    def turn_row(row, carry):
        for c in range(COLS):
            turn(row * PLACES + c, carry)
        return carry

    lax.fori_loop(0, ROWS, turn_row, 0)

    def distances(cell, slot):
        table = irows[pl.ds(pl.multiple_of(cell * DEPTH, DEPTH), DEPTH), :]
        for n, (a, b) in enumerate(NEIGHBOURS):
            right_side = (table * scales[0, n]).astype(BF16)
            dist[slot, n] = jnp.dot(
                jcols[cell + a * PLACES + b], right_side, preferred_element_type=F32
            )

    def cell_of(n, columns, row0, column0):
        return (n // columns + row0) * PLACES + n % columns + column0

    def density_of(n, carry):
        cell = cell_of(n, 10, 1, 1)
        distances(cell_of(jnp.minimum(n + 1, 39), 10, 1, 1), (n + 1) % 2)
        slot = n % 2
        total = jnp.zeros((8, 128), F32)
        for m, (a, b) in enumerate(NEIGHBOURS):
            near = cell + a * PLACES + b
            for at in range(0, 128, 32):
                y = jnp.maximum(dist[slot, m, at : at + 32, :], 1e-12)
                q = y * lax.rsqrt(y)
                reach = jnp.maximum(2.0 - q, 0.0)
                inner = 4.0 - 3.0 * y * reach
                outer = reach * reach * reach
                w = jnp.where(y < 1.0, inner, outer) * masses[near, at : at + 32, :]
                total = total + ((w[0:8] + w[8:16]) + (w[16:24] + w[24:32]))
        rho = jnp.sum(total, axis=0, keepdims=True) * (0.25 * KERNEL_NORM)
        rhos[pl.ds(cell, 1), :] = rho
        return carry

    distances(cell_of(0, 10, 1, 1), 0)
    lax.fori_loop(0, 40, density_of, 0)

    def coefficients(step, carry):
        row, half = step // 2 + 1, step % 2
        base = (row * 2 + half) * (8 * DEPTH)
        cells = pl.ds(pl.multiple_of(half * 8, 8), 8)
        mass = fields[row, 6, cells, :]
        rho = rhos[pl.ds(pl.multiple_of(row * PLACES + half * 8, 8), 8), :]
        share = mass / jnp.where(mass > 0.0, rho, 1.0)
        terms = []
        for weight in (mass, share):
            terms.append(weight)
            for f in range(3):
                high, low = parts_of(2.0 * fields[row, f, cells, :] - 1.0, 2)
                terms.append(weight * (high + low))
            terms.append(weight)
            terms.append(weight)
        for f in range(3, 6):
            terms.append(share * fields[row, f, cells, :])
        terms.append(jnp.zeros((8, 128), F32))
        for t, term in enumerate(terms):
            high, low = parts_of(term, 2)
            crows[pl.ds(base + t, 8, stride=DEPTH), :] = high
            crows[pl.ds(base + 16 + t, 8, stride=DEPTH), :] = low
        return carry

    lax.fori_loop(0, 8, coefficients, 0)

    def force_of(n, carry):
        cell = cell_of(n, 8, 2, 2)
        distances(cell_of(jnp.minimum(n + 1, 15), 8, 2, 2), (n + 1) % 2)
        slot = n % 2
        total = jnp.zeros((DEPTH, 256), F32)
        for m, (a, b) in enumerate(NEIGHBOURS):
            near = cell + a * PLACES + b
            table = crows[pl.ds(pl.multiple_of(near * DEPTH, DEPTH), DEPTH), :]
            left_side = (table * scales[1, m]).astype(BF16)
            highs, lows = [], []
            for at in range(0, 128, 32):
                y = jnp.maximum(dist[slot, m, at : at + 32, :], 1e-12)
                inverse = lax.rsqrt(y)
                q = y * inverse
                reach = jnp.maximum(2.0 - q, 0.0)
                slope = jnp.where(y < 1.0, 4.0 - 3.0 * q, reach * reach * inverse)
                soft = lax.rsqrt(y + 4.0 * SOFTENING)
                damped = slope * (y * (soft * soft))
                both = jnp.concatenate([slope, damped], axis=1)
                high = both.astype(BF16)
                highs.append(high)
                lows.append((both - high.astype(F32)).astype(BF16))
            total = total + jnp.dot(
                left_side, jnp.concatenate(highs, axis=0), preferred_element_type=F32
            )
            total = total + jnp.dot(
                left_side, jnp.concatenate(lows, axis=0), preferred_element_type=F32
            )
        total = total[0:16] + total[16:32]
        for half in range(2):
            at = pl.ds(pl.multiple_of(n * 16, 16), 16)
            sums[half, at, :] = total[:, 128 * half : 128 * (half + 1)]
        return carry

    distances(cell_of(0, 8, 2, 2), 0)
    lax.fori_loop(0, 16, force_of, 0)

    for row in range(2):
        mass = fields[2 + row, 6, 2:10, :]
        valid = mass > 0.0
        rho = rhos[(2 + row) * PLACES + 2 : (2 + row) * PLACES + 10, :]
        density[row] = jnp.where(valid, rho, 0.0)
        inverse_rho = 1.0 / jnp.where(valid, rho, 1.0)

        def term(k, half):
            return sums[half, pl.ds(row * 128 + k, 8, stride=16), :]

        mass_sum, share_sum, drag_sum = term(0, 0), term(6, 0), term(6, 1)
        pressure_scale = -3.0 * KERNEL_NORM * -SOUND_SQ * 0.5
        viscous_scale = -3.0 * KERNEL_NORM * 2.0 * VISCOSITY
        for f in range(3):
            high, low = parts_of(2.0 * fields[2 + row, f, 2:10, :] - 1.0, 2)
            x = high + low
            first = x * mass_sum - term(1 + f, 0)
            second = x * share_sum - term(7 + f, 0)
            if f < 2:
                first = first - 2.0 * term(4 + f, 0)
                second = second - 2.0 * term(10 + f, 0)
            viscous = fields[2 + row, 3 + f, 2:10, :] * drag_sum - term(12 + f, 1)
            value = pressure_scale * (first * inverse_rho + second)
            value = value + viscous_scale * viscous * inverse_rho
            accel[row, f] = jnp.where(valid, value, 0.0)


def local(rows_axis, columns_axis, position, velocity, particle_mass, cell_counts, shear_shift):
    slabs, blocks = lax.axis_size(rows_axis), lax.axis_size(columns_axis)
    axes = (rows_axis, columns_axis)
    half = blocks // 2
    slab = lax.axis_index(rows_axis)
    past = shear_shift[0] - half * particle_mass.shape[1]

    fields = pl.pallas_call(
        pack_kernel,
        out_shape=jax.ShapeDtypeStruct((2, 7, 8, 128), F32),
        in_specs=[SMEM, VMEM, VMEM, VMEM],
        out_specs=VMEM,
        name="pack",
    )(
        cell_counts,
        jnp.transpose(position, (0, 3, 1, 2)),
        jnp.transpose(velocity, (0, 3, 1, 2)),
        particle_mass,
    )
    ring = [(i, (i + 1) % blocks) for i in range(blocks)]
    left = lax.ppermute(fields, columns_axis, ring)
    right = lax.ppermute(fields, columns_axis, [(j, i) for i, j in ring])

    odd = lax.rem(slab, 2)
    start = 6 + jnp.where(slab == slabs - 1, past, jnp.where(slab == 0, -past, 0))
    info = jnp.stack([odd, start]).astype(jnp.int32)
    sent = jax.ShapeDtypeStruct((SENT, 128), F32)
    same, far = pl.pallas_call(
        window_kernel,
        out_shape=(sent, sent),
        in_specs=[SMEM, VMEM, VMEM, VMEM],
        out_specs=(VMEM, VMEM),
        name="window",
    )(info, left, fields, right)

    same_pairs, far_pairs = [], []
    for s in range(slabs):
        for b in range(blocks):
            me = s * blocks + b
            same_pairs.append((me, (s + 1 if s % 2 == 0 else s - 1) * blocks + b))
            other, to = (s - 1, b) if s % 2 == 0 else (s + 1, b)
            if other < 0 or other >= slabs:
                other, to = other % slabs, (b + half) % blocks
            far_pairs.append((me, other * blocks + to))
    far = lax.ppermute(far, axes, far_pairs)
    same = lax.ppermute(same, axes, same_pairs)

    jump = jnp.where(slab == slabs - 1, SHEAR_JUMP, jnp.where(slab == 0, -SHEAR_JUMP, 0.0))
    cells = ROWS * PLACES
    density, accel = pl.pallas_call(
        main_kernel,
        out_shape=(
            jax.ShapeDtypeStruct((2, 8, 128), F32),
            jax.ShapeDtypeStruct((2, 3, 8, 128), F32),
        ),
        in_specs=[SMEM, SMEM] + [VMEM] * 5,
        out_specs=(VMEM, VMEM),
        scratch_shapes=[
            pltpu.VMEM((ROWS, 7, PLACES, 128), F32),
            pltpu.VMEM((cells * DEPTH, 128), F32),
            pltpu.VMEM((cells * DEPTH, 128), F32),
            pltpu.VMEM((cells * DEPTH, 128), F32),
            pltpu.VMEM((cells, 128, DEPTH), BF16),
            pltpu.VMEM((cells, 128, 128), F32),
            pltpu.VMEM((2, 9, DEPTH, 128), F32),
            pltpu.VMEM((cells, 128), F32),
            pltpu.VMEM((2, 9, 128, 128), F32),
            pltpu.VMEM((2, 16 * 16, 128), F32),
        ],
        name="particles",
    )(info, jump.astype(F32)[None], left, fields, right, same, far)
    return (density, jnp.transpose(accel, (0, 2, 3, 1)))


def solution(mesh):
    placed = (
        P("gy", "gx", None, None),
        P("gy", "gx", None, None),
        P("gy", "gx", None),
        P("gy", "gx"),
        P(),
    )
    return jax.shard_map(
        functools.partial(local, "gy", "gx"),
        mesh=mesh,
        in_specs=placed,
        out_specs=(P("gy", "gx", None), P("gy", "gx", None, None)),
        check_vma=False,
    )
```

time: 135 us -> 81.5 us (0.60)
  the two profiles are of different devices: /device:TPU:191 before, /device:TPU:7 now
where the time goes in v1:
time: 81.5 us; the launch traced here: 81.1 us
  Pallas kernels  41.1 us (50%)
  starting transfers between devices  21.4 us (26%)
  waiting for transfers between devices  15.4 us (19%)
  between operations  1.36 us (2%)
  local copies, waits for them, and re-layouts  1.24 us (2%)
    pallas_call x1, Pallas kernels, local(): pl.pallas_call(main_kernel, out_shape=(jax.ShapeDtypeStruct((2, 8, 128),...  38.1 us
    ppermute x1, starting transfers between devices, local(): right = lax.ppermute(fields, columns_axis, [(j, i) for i, j in ring])  13.6 us
    ppermute x1, waiting for transfers between devices, local(): far = lax.ppermute(far, axes, far_pairs)  10.2 us
    ppermute x1, waiting for transfers between devices, local(): left = lax.ppermute(fields, columns_axis, ring)  5.19 us
    ppermute x1, starting transfers between devices, local(): same = lax.ppermute(same, axes, same_pairs)  4 us
    ppermute x1, starting transfers between devices, local(): left = lax.ppermute(fields, columns_axis, ring)  1.92 us
    ppermute x1, starting transfers between devices, local(): far = lax.ppermute(far, axes, far_pairs)  1.92 us
  transfers between devices with their start and end apart: 4, of which 2 were waited for; matrix products, arithmetic and copies ran while one was open for 1% of the time, Pallas kernels for 0%

profile of v1, /device:TPU:7, one launch (start us, length us, event | category | flops | bytes accessed | tf_op | source)
XLA Modules:
  0.0 81.1 jit_solution(11033392872085276685)
XLA Ops:
  0.6 1.5 %pack.1.own = f32[2,7,8,128]{3,2,1,0:T(8,128)} custom-call(s32[2,8]{1,0:T(2,128)} %counts.1, f32[2,3,8,128]{3,2,1,0:T(8,128)} %bitcast.7, f32[2,3,8,128]{3,2,1,0:T(8,128)} %bitcast.8, f32[2,8,128]{2,1,0:T(8,128)} %mass.1), custom_call_target="tpu_custom_call" | custom-call | tf_op jit(solution)/shard_map/pack/pallas_call | solution.py:298
  2.1 13.6 %collective-permute-start.1 = (f32[2,7,8,128]{3,2,1,0:T(8,128)}, f32[2,7,8,128]{3,2,1,0:T(8,128)S(1)}, u32[]{:S(2)}, u32[]{:S(2)}) collective-permute-start(f32[2,7,8,128]{3,2,1,0:T(8,128)} %pack.1.own), channel_id=1, source_target_pairs={{1,0},{2,1},{3,2},{4,3},{5,4},{6,5},{7,6},{8,7},{9,8},{10,9},{11,1... | collective-permute-start | bytes 172040 | tf_op jit(solution)/shard_map/ppermute | solution.py:312
  15.7 1.9 %collective-permute-start = (f32[2,7,8,128]{3,2,1,0:T(8,128)}, f32[2,7,8,128]{3,2,1,0:T(8,128)S(1)}, u32[]{:S(2)}, u32[]{:S(2)}) collective-permute-start(f32[2,7,8,128]{3,2,1,0:T(8,128)} %pack.1.own), channel_id=1, source_target_pairs={{0,1},{1,2},{2,3},{3,4},{4,5},{5,6},{6,7},{7,8},{8,9},{9,10},{10,1... | collective-permute-start | bytes 172040 | tf_op jit(solution)/shard_map/ppermute | solution.py:311
  18.3 0.7 pad_add_fusion.info
  18.9 0.0 collective-permute-done.1.right
  18.9 0.0 copy-start
  18.9 5.2 %collective-permute-done.left = f32[2,7,8,128]{3,2,1,0:T(8,128)S(1)} collective-permute-done((f32[2,7,8,128]{3,2,1,0:T(8,128)}, f32[2,7,8,128]{3,2,1,0:T(8,128)S(1)}, u32[]{:S(2)}, u32[]{:S(2)}) %collective-permute-start) | collective-permute-done | bytes 57376 | tf_op jit(solution)/shard_map/ppermute | solution.py:311
  24.1 0.0 copy-done
  24.1 0.0 copy-start.1
  24.1 0.6 copy-done.1
  24.7 1.5 %window.1 = (f32[136,128]{1,0:T(8,128)}, f32[136,128]{1,0:T(8,128)}) custom-call(s32[2]{0:T(128)} %pad_add_fusion.info, f32[2,7,8,128]{3,2,1,0:T(8,128)} %copy-done.1, f32[2,7,8,128]{3,2,1,0:T(8,128)} %pack.1.own, f32[2,7,8,128]{3,2,1,0:T(8,128)} %copy-done), custom_call_target="tpu_custom_call" | custom-call | tf_op jit(solution)/shard_map/window/pallas_call | solution.py:318
  26.3 4.0 %collective-permute-start.2 = (f32[136,128]{1,0:T(8,128)}, f32[136,128]{1,0:T(8,128)S(1)}, u32[]{:S(2)}, u32[]{:S(2)}) collective-permute-start(f32[136,128]{1,0:T(8,128)} %get-tuple-element.6), channel_id=1, source_target_pairs={{0,64},{1,65},{2,66},{3,67},{4,68},{5,69},{6,70},{7,71},{8,72},{9,... | collective-permute-start | bytes 208904 | tf_op jit(solution)/shard_map/ppermute | solution.py:336
  30.3 1.9 %collective-permute-start.3 = (f32[136,128]{1,0:T(8,128)}, f32[136,128]{1,0:T(8,128)S(1)}, u32[]{:S(2)}, u32[]{:S(2)}) collective-permute-start(f32[136,128]{1,0:T(8,128)} %get-tuple-element.7), channel_id=1, source_target_pairs={{0,480},{1,481},{2,482},{3,483},{4,484},{5,485},{6,486},{7,487},{8... | collective-permute-start | bytes 208904 | tf_op jit(solution)/shard_map/ppermute | solution.py:335
  32.2 0.0 collective-permute-done.2.same
  32.2 0.0 copy-start.2
  32.2 10.2 %collective-permute-done.3.far = f32[136,128]{1,0:T(8,128)S(1)} collective-permute-done((f32[136,128]{1,0:T(8,128)}, f32[136,128]{1,0:T(8,128)S(1)}, u32[]{:S(2)}, u32[]{:S(2)}) %collective-permute-start.3) | collective-permute-done | bytes 69664 | tf_op jit(solution)/shard_map/ppermute | solution.py:335
  42.4 0.0 copy-start.3
  42.4 0.0 copy-done.2
  42.4 0.6 copy-done.3
  43.0 38.1 %particles.1 = (f32[2,8,128]{2,1,0:T(8,128)}, f32[2,3,8,128]{3,2,1,0:T(8,128)}) custom-call(s32[2]{0:T(128)} %pad_add_fusion.info, f32[1]{0:T(128)} %bitcast.3.jump_ref, f32[2,7,8,128]{3,2,1,0:T(8,128)} %copy-done.1, f32[2,7,8,128]{3,2,1,0:T(8,128)} %pack.1.own, f32[2,7,8,128]{3,2,1,0:T(8,128)} %copy-done, f32[136,128]{1,0:T(8,128)} %copy-done.2, ...), custom_call_target="tpu_custom_call" | custom-call | tf_op jit(solution)/shard_map/particles/pallas_call | solution.py:340
Async XLA Ops:
  2.1 16.8 %collective-permute-start.1 = (f32[2,7,8,128]{3,2,1,0:T(8,128)}, f32[2,7,8,128]{3,2,1,0:T(8,128)S(1)}, u32[]{:S(2)}, u32[]{:S(2)}) collective-permute-start(f32[2,7,8,128]{3,2,1,0:T(8,128)} %pack.1.own), channel_id=1, source_target_pairs={{1,0},{2,1},{3,2},{4,3},{5,4},{6,5},{7,6},{8,7},{9,8},{10,9},{11,1... | collective-permute-start | bytes 172040 | tf_op jit(solution)/shard_map/ppermute | solution.py:312
  15.7 8.5 %collective-permute-start = (f32[2,7,8,128]{3,2,1,0:T(8,128)}, f32[2,7,8,128]{3,2,1,0:T(8,128)S(1)}, u32[]{:S(2)}, u32[]{:S(2)}) collective-permute-start(f32[2,7,8,128]{3,2,1,0:T(8,128)} %pack.1.own), channel_id=1, source_target_pairs={{0,1},{1,2},{2,3},{3,4},{4,5},{5,6},{6,7},{7,8},{8,9},{9,10},{10,1... | collective-permute-start | bytes 172040 | tf_op jit(solution)/shard_map/ppermute | solution.py:311
  18.9 5.2 %copy-start = (f32[2,7,8,128]{3,2,1,0:T(8,128)}, f32[2,7,8,128]{3,2,1,0:T(8,128)S(1)}, u32[]{:S(2)}) copy-start(f32[2,7,8,128]{3,2,1,0:T(8,128)S(1)} %collective-permute-done.1.right) | copy-start | bytes 172036
  24.1 0.6 copy-start.1
  26.3 5.9 %collective-permute-start.2 = (f32[136,128]{1,0:T(8,128)}, f32[136,128]{1,0:T(8,128)S(1)}, u32[]{:S(2)}, u32[]{:S(2)}) collective-permute-start(f32[136,128]{1,0:T(8,128)} %get-tuple-element.6), channel_id=1, source_target_pairs={{0,64},{1,65},{2,66},{3,67},{4,68},{5,69},{6,70},{7,71},{8,72},{9,... | collective-permute-start | bytes 208904 | tf_op jit(solution)/shard_map/ppermute | solution.py:336
  30.3 12.1 %collective-permute-start.3 = (f32[136,128]{1,0:T(8,128)}, f32[136,128]{1,0:T(8,128)S(1)}, u32[]{:S(2)}, u32[]{:S(2)}) collective-permute-start(f32[136,128]{1,0:T(8,128)} %get-tuple-element.7), channel_id=1, source_target_pairs={{0,480},{1,481},{2,482},{3,483},{4,484},{5,485},{6,486},{7,487},{8... | collective-permute-start | bytes 208904 | tf_op jit(solution)/shard_map/ppermute | solution.py:335
  32.2 10.2 %copy-start.2 = (f32[136,128]{1,0:T(8,128)}, f32[136,128]{1,0:T(8,128)S(1)}, u32[]{:S(2)}) copy-start(f32[136,128]{1,0:T(8,128)S(1)} %collective-permute-done.2.same) | copy-start | bytes 208900
  42.4 0.6 copy-start.3

commit v2 on v1

v2 whole, which is shorter than its diff:
```python
import functools
import math

import jax
import jax.numpy as jnp
from jax import lax
from jax.experimental import pallas as pl
from jax.experimental.pallas import tpu as pltpu
from jax.sharding import PartitionSpec as P

SMOOTHING = 0.5
KERNEL_NORM = 1.0 / (math.pi * SMOOTHING**3)
SOUND_SQ = 0.2
VISCOSITY = 0.05
SOFTENING = 0.0025
SHEAR_JUMP = 1.0

COLS, PLACES = 12, 16
DEPTH = 32
NEAR, FAR = 7, 4
SENT = 136
BF16, F32 = jnp.bfloat16, jnp.float32
NEIGHBOURS = [(a, b) for a in (-1, 0, 1) for b in (-1, 0, 1)]
VMEM = pl.BlockSpec(memory_space=pltpu.VMEM)
SMEM = pl.BlockSpec(memory_space=pltpu.SMEM)
HBM = pl.BlockSpec(memory_space=pltpu.HBM)
TABLES = (
    jax.ShapeDtypeStruct((2, 7, PLACES, 128), F32),
    jax.ShapeDtypeStruct((2 * PLACES * DEPTH, 128), F32),
    jax.ShapeDtypeStruct((2 * PLACES, 128, DEPTH), BF16),
    jax.ShapeDtypeStruct((2 * PLACES, 128, 128), F32),
)


def pack_kernel(counts, pos_hbm, vel_hbm, mass_hbm, out, pos, vel, mass, sems):
    copies = [
        pltpu.make_async_copy(source, to, sems.at[n])
        for n, (source, to) in enumerate(((pos_hbm, pos), (vel_hbm, vel), (mass_hbm, mass)))
    ]
    for copy in copies:
        copy.start()
    slot = lax.broadcasted_iota(jnp.int32, (8, 128), 1)
    column = lax.broadcasted_iota(jnp.int32, (8, 128), 0)
    limits = []
    for row in range(2):
        limit = jnp.zeros((8, 128), jnp.int32)
        for c in range(8):
            limit = jnp.where(column == c, counts[row, c], limit)
        limits.append(limit)
    for copy in copies:
        copy.wait()
    for row in range(2):
        out[row, 0:3] = pos[row]
        out[row, 3:6] = vel[row]
        out[row, 6] = jnp.where(slot < limits[row], mass[row], 0.0)


def window_kernel(info, left, own, right, far_out, same_out):
    odd, start = info[0], info[1]
    for out in (far_out, same_out):
        near_row = jnp.where(odd == 1, 1, 0)
        if out is same_out:
            near_row = 1 - near_row
        place = 0
        for row, fields in ((near_row, range(NEAR)), (1 - near_row, (0, 1, 2, 6))):
            for f in fields:
                wide = jnp.concatenate([left[row, f], own[row, f], right[row, f]], axis=0)
                if out is same_out:
                    piece = wide[6:18]
                else:
                    piece = pltpu.roll(wide, 24 - start, 0)[0:COLS]
                out[place : place + COLS, :] = piece
                place += COLS
        out[place:SENT, :] = jnp.zeros((SENT - place, 128), F32)


def parts_of(x, count):
    parts = []
    for _ in range(count - 1):
        part = x.astype(BF16).astype(F32)
        parts.append(part)
        x = x - part
    parts.append(x.astype(BF16).astype(F32))
    return parts


def fill_scales(scales):
    k = lax.broadcasted_iota(jnp.int32, (DEPTH, 128), 0)
    for n, (a, b) in enumerate(NEIGHBOURS):
        scale = jnp.where(k < 18, 1.0, 0.0)
        scale = jnp.where((k >= 18) & (k < 22), float(b), scale)
        scale = jnp.where((k >= 22) & (k < 26), float(a), scale)
        scale = jnp.where(k == 26, float(a * a + b * b), scale)
        scales[0, n] = scale
        if scales.shape[0] > 1:
            scale = jnp.where((k == 4) | (k == 10) | (k == 20) | (k == 26), float(b), 1.0)
            scale = jnp.where((k == 5) | (k == 11) | (k == 21) | (k == 27), float(a), scale)
            scales[1, n] = scale


def build_tables(rows, fields, irows, jcols, masses, jrows):
    k = lax.broadcasted_iota(jnp.int32, (DEPTH, 128), 0)
    ones_j = jnp.where(((k >= 15) & (k < 20)) | (k == 22) | (k == 23) | (k == 26), 1.0, 0.0)
    ones_i = jnp.where((k >= 12) & (k < 15), 1.0, 0.0)
    ones_i = jnp.where((k == 20) | (k == 21) | (k >= 24) & (k < 27), 4.0, ones_i)
    pick_mass = jnp.where((k >= 27) & (k < 30), 1.0, 0.0).astype(BF16)

    def build(step, carry):
        row, half = step // 2, step % 2
        base = pl.multiple_of(step * (8 * DEPTH), 8 * DEPTH)
        cells = pl.ds(pl.multiple_of(half * 8, 8), 8)
        for c in range(8):
            jrows[pl.ds(base + c * DEPTH, DEPTH), :] = ones_j
            irows[pl.ds(base + c * DEPTH, DEPTH), :] = ones_i

        def put(table, k, value):
            table[pl.ds(base + k, 8, stride=DEPTH), :] = value

        norm = jnp.zeros((8, 128), F32)
        for f in range(3):
            x = 2.0 * fields[row, f, cells, :] - 1.0
            high, low = parts_of(x, 2)
            both = high + low
            norm = norm + both * both
            for k, (mine, other) in enumerate(((high, high), (high, low), (low, high), (low, low))):
                put(jrows, 4 * f + k, mine)
                put(irows, 4 * f + k, -2.0 * other)
            if f < 2:
                at = 18 + 4 * f
                put(jrows, at + 2, high)
                put(jrows, at + 3, low)
                put(irows, at, -4.0 * high)
                put(irows, at + 1, -4.0 * low)
        for k, part in enumerate(parts_of(norm, 3)):
            put(jrows, 12 + k, part)
            put(irows, 15 + k, part)
        for k, part in enumerate(parts_of(fields[row, 6, cells, :], 3)):
            put(jrows, 27 + k, part)
        return carry

    lax.fori_loop(0, rows * 2, build, 0)

    def turn_row(row, carry):
        for c in range(COLS):
            cell = row * PLACES + c
            table = jrows[pl.ds(pl.multiple_of(cell * DEPTH, DEPTH), DEPTH), :]
            flipped = table.T.astype(BF16)
            jcols[cell] = flipped
            masses[cell] = jnp.dot(flipped, pick_mass, preferred_element_type=F32)
        return carry

    lax.fori_loop(0, rows, turn_row, 0)


def rows_of(table, cell):
    return table[pl.ds(pl.multiple_of(cell * DEPTH, DEPTH), DEPTH), :]


def put_distances(dist, m, table, scale, columns):
    right_side = (table * scale).astype(BF16)
    dist[m] = jnp.dot(columns, right_side, preferred_element_type=F32)


def add_density(total, dist, m, masses, cell):
    for at in range(0, 128, 32):
        y = jnp.maximum(dist[m, at : at + 32, :], 1e-12)
        q = y * lax.rsqrt(y)
        reach = jnp.maximum(2.0 - q, 0.0)
        inner = 4.0 - 3.0 * y * reach
        outer = reach * reach * reach
        w = jnp.where(y < 1.0, inner, outer) * masses[cell, at : at + 32, :]
        total = total + ((w[0:8] + w[8:16]) + (w[16:24] + w[24:32]))
    return total


def density_of(total):
    return jnp.sum(total, axis=0, keepdims=True) * (0.25 * KERNEL_NORM)


def row_index(direction, b):
    return direction * 3 + b + 1


def early_kernel(left, own, right, fields, irows, jcols, masses, rhos, jrows, scales, dist):
    fields[...] = jnp.zeros_like(fields)
    for row in range(2):
        for f in range(7):
            fields[row, f, 0:2, :] = left[row, f, 6:8, :]
            fields[row, f, 2:10, :] = own[row, f]
            fields[row, f, 10:12, :] = right[row, f, 0:2, :]
    fill_scales(scales)
    build_tables(2, fields, irows, jcols, masses, jrows)

    def blocks(n):
        side, column = n // 10, n % 10 + 1
        cell = side * PLACES + column
        other = (1 - side) * PLACES + column
        return cell, [
            (row_index(direction, b), at + b)
            for direction, at in ((1, cell), (2 - 2 * side, other))
            for b in (-1, 0, 1)
        ]

    def measure(n, m):
        cell, near = blocks(n)
        put_distances(dist, m, rows_of(irows, cell), scales[0, near[m][0]], jcols[near[m][1]])

    def step(n, carry):
        cell, near = blocks(n)
        following = jnp.minimum(n + 1, 19)
        total = jnp.zeros((8, 128), F32)
        for m in range(6):
            total = add_density(total, dist, m, masses, near[m][1])
            measure(following, m)
        rhos[pl.ds(cell, 1), :] = density_of(total)
        return carry

    rhos[...] = jnp.zeros_like(rhos)
    for m in range(6):
        measure(0, m)
    lax.fori_loop(0, 20, step, 0)


def late_kernel(
    info, jump_ref, far, same, fields, irows, jcols, masses, partial, density, accel,
    ghosts, ghost_irows, ghost_jcols, ghost_masses, jrows,
    scales, rhos, ghost_rhos, crows, ghost_crows, dist, sums,
):
    odd, jump = info[0], jump_ref[0]

    ghosts[...] = jnp.zeros_like(ghosts)
    for piece, side in ((same, 1 - odd), (far, odd)):
        for f in range(NEAR):
            value = piece[f * COLS : (f + 1) * COLS, :]
            if piece is far and f == 3:
                value = value + jump
            ghosts[side, f, 0:COLS, :] = value
        for n, f in enumerate((0, 1, 2, 6)):
            at = (NEAR + n) * COLS
            ghosts[2 + side, f, 0:COLS, :] = piece[at : at + COLS, :]
    fill_scales(scales)
    build_tables(4, ghosts, ghost_irows, ghost_jcols, ghost_masses, jrows)

    def blocks(n):
        side, column = n // 10, n % 10 + 1
        cell = side * PLACES + column
        return cell, side, [
            (who, row_index(direction, b), at + b)
            for who, direction, at in (
                ("far", 2 * side, cell + 2 * PLACES),
                ("near", 1, cell),
                ("own", 2 - 2 * side, cell),
                ("mine", 2 * side, cell),
            )
            for b in (-1, 0, 1)
        ]

    def measure(n, m):
        cell, side, near = blocks(n)
        who, index, at = near[m]
        table = rows_of(irows if who == "mine" else ghost_irows, cell)
        columns = (jcols if who == "own" else ghost_jcols)[at]
        put_distances(dist, m, table, scales[0, index], columns)

    def density_step(n, carry):
        cell, side, near = blocks(n)
        following = jnp.minimum(n + 1, 19)
        ghost_total = jnp.zeros((8, 128), F32)
        own_total = jnp.zeros((8, 128), F32)
        for m in range(12):
            who, index, at = near[m]
            which = masses if who == "own" else ghost_masses
            if who == "mine":
                own_total = add_density(own_total, dist, m, which, at)
            else:
                ghost_total = add_density(ghost_total, dist, m, which, at)
            measure(following, m)
        ghost_rhos[pl.ds(cell, 1), :] = density_of(ghost_total)
        rhos[pl.ds(cell, 1), :] = density_of(own_total) + partial[pl.ds(cell, 1), :]
        return carry

    rhos[...] = jnp.zeros_like(rhos)
    ghost_rhos[...] = jnp.zeros_like(ghost_rhos)
    for m in range(12):
        measure(0, m)
    lax.fori_loop(0, 20, density_step, 0)

    def coefficients(source, densities, target):
        def step(n, carry):
            row, half = n // 2, n % 2
            base = n * (8 * DEPTH)
            cells = pl.ds(pl.multiple_of(half * 8, 8), 8)
            mass = source[row, 6, cells, :]
            rho = densities[pl.ds(pl.multiple_of(n * 8, 8), 8), :]
            share = mass / jnp.where(mass > 0.0, rho, 1.0)
            terms = []
            for weight in (mass, share):
                terms.append(weight)
                for f in range(3):
                    high, low = parts_of(2.0 * source[row, f, cells, :] - 1.0, 2)
                    terms.append(weight * (high + low))
                terms.append(weight)
                terms.append(weight)
            for f in range(3, 6):
                terms.append(share * source[row, f, cells, :])
            terms.append(jnp.zeros((8, 128), F32))
            for t, term in enumerate(terms):
                high, low = parts_of(term, 2)
                target[pl.ds(base + t, 8, stride=DEPTH), :] = high
                target[pl.ds(base + 16 + t, 8, stride=DEPTH), :] = low
            return carry

        lax.fori_loop(0, 4, step, 0)

    coefficients(fields, rhos, crows)
    coefficients(ghosts, ghost_rhos, ghost_crows)

    def force_blocks(n):
        side, column = n // 8, n % 8 + 2
        cell = side * PLACES + column
        other = (1 - side) * PLACES + column
        return cell, [
            (ghost, row_index(direction, b), at + b)
            for ghost, direction, at in (
                (True, 2 * side, cell),
                (False, 1, cell),
                (False, 2 - 2 * side, other),
            )
            for b in (-1, 0, 1)
        ]

    def force_measure(n, m):
        cell, near = force_blocks(n)
        ghost, index, at = near[m]
        columns = (ghost_jcols if ghost else jcols)[at]
        put_distances(dist, m, rows_of(irows, cell), scales[0, index], columns)

    def force_step(n, carry):
        cell, near = force_blocks(n)
        following = jnp.minimum(n + 1, 15)
        total = jnp.zeros((DEPTH, 256), F32)
        for m in range(9):
            ghost, index, at = near[m]
            table = rows_of(ghost_crows if ghost else crows, at)
            left_side = (table * scales[1, index]).astype(BF16)
            highs, lows = [], []
            for at in range(0, 128, 32):
                y = jnp.maximum(dist[m, at : at + 32, :], 1e-12)
                inverse = lax.rsqrt(y)
                q = y * inverse
                reach = jnp.maximum(2.0 - q, 0.0)
                slope = jnp.where(y < 1.0, 4.0 - 3.0 * q, reach * reach * inverse)
                soft = lax.rsqrt(y + 4.0 * SOFTENING)
                damped = slope * (y * (soft * soft))
                both = jnp.concatenate([slope, damped], axis=1)
                high = both.astype(BF16)
                highs.append(high)
                lows.append((both - high.astype(F32)).astype(BF16))
            force_measure(following, m)
            total = total + jnp.dot(
                left_side, jnp.concatenate(highs, axis=0), preferred_element_type=F32
            )
            total = total + jnp.dot(
                left_side, jnp.concatenate(lows, axis=0), preferred_element_type=F32
            )
        total = total[0:16] + total[16:32]
        for half in range(2):
            at = pl.ds(pl.multiple_of(n * 16, 16), 16)
            sums[half, at, :] = total[:, 128 * half : 128 * (half + 1)]
        return carry

    for m in range(9):
        force_measure(0, m)
    lax.fori_loop(0, 16, force_step, 0)

    for row in range(2):
        mass = fields[row, 6, 2:10, :]
        valid = mass > 0.0
        rho = rhos[row * PLACES + 2 : row * PLACES + 10, :]
        density[row] = jnp.where(valid, rho, 0.0)
        inverse_rho = 1.0 / jnp.where(valid, rho, 1.0)

        def term(k, half):
            return sums[half, pl.ds(row * 128 + k, 8, stride=16), :]

        mass_sum, share_sum, drag_sum = term(0, 0), term(6, 0), term(6, 1)
        pressure_scale = -3.0 * KERNEL_NORM * -SOUND_SQ * 0.5
        viscous_scale = -3.0 * KERNEL_NORM * 2.0 * VISCOSITY
        for f in range(3):
            high, low = parts_of(2.0 * fields[row, f, 2:10, :] - 1.0, 2)
            x = high + low
            first = x * mass_sum - term(1 + f, 0)
            second = x * share_sum - term(7 + f, 0)
            if f < 2:
                first = first - 2.0 * term(4 + f, 0)
                second = second - 2.0 * term(10 + f, 0)
            viscous = fields[row, 3 + f, 2:10, :] * drag_sum - term(12 + f, 1)
            value = pressure_scale * (first * inverse_rho + second)
            value = value + viscous_scale * viscous * inverse_rho
            accel[row, f] = jnp.where(valid, value, 0.0)


def scratch_of(tables, rows):
    return [
        pltpu.VMEM((t.shape[0] // 2 * rows, *t.shape[1:]), t.dtype) for t in tables
    ]


def params(mib):
    return pltpu.CompilerParams(vmem_limit_bytes=mib * 2**20)


def local(rows_axis, columns_axis, position, velocity, particle_mass, cell_counts, shear_shift):
    slabs, blocks = lax.axis_size(rows_axis), lax.axis_size(columns_axis)
    axes = (rows_axis, columns_axis)
    half = blocks // 2
    slab = lax.axis_index(rows_axis)
    past = shear_shift[0] - half * particle_mass.shape[1]

    fields = pl.pallas_call(
        pack_kernel,
        out_shape=jax.ShapeDtypeStruct((2, 7, 8, 128), F32),
        in_specs=[SMEM, HBM, HBM, HBM],
        out_specs=VMEM,
        scratch_shapes=[
            pltpu.VMEM((2, 3, 8, 128), F32),
            pltpu.VMEM((2, 3, 8, 128), F32),
            pltpu.VMEM((2, 8, 128), F32),
            pltpu.SemaphoreType.DMA((3,)),
        ],
        name="pack",
    )(
        cell_counts,
        jnp.transpose(position, (0, 3, 1, 2)),
        jnp.transpose(velocity, (0, 3, 1, 2)),
        particle_mass,
    )
    ring = [(i, (i + 1) % blocks) for i in range(blocks)]
    left = lax.ppermute(fields, columns_axis, ring)
    right = lax.ppermute(fields, columns_axis, [(j, i) for i, j in ring])

    odd = lax.rem(slab, 2)
    start = 6 + jnp.where(slab == slabs - 1, past, jnp.where(slab == 0, -past, 0))
    info = jnp.stack([odd, start]).astype(jnp.int32)
    sent = jax.ShapeDtypeStruct((SENT, 128), F32)
    far, same = pl.pallas_call(
        window_kernel,
        out_shape=(sent, sent),
        in_specs=[SMEM, VMEM, VMEM, VMEM],
        out_specs=(VMEM, VMEM),
        compiler_params=params(4),
        name="window",
    )(info, left, fields, right)

    same_pairs, far_pairs = [], []
    for s in range(slabs):
        for b in range(blocks):
            me = s * blocks + b
            same_pairs.append((me, (s + 1 if s % 2 == 0 else s - 1) * blocks + b))
            other, to = (s - 1, b) if s % 2 == 0 else (s + 1, b)
            if other < 0 or other >= slabs:
                other, to = other % slabs, (b + half) % blocks
            far_pairs.append((me, other * blocks + to))
    far = lax.ppermute(far, axes, far_pairs)
    same = lax.ppermute(same, axes, same_pairs)

    tables = pl.pallas_call(
        early_kernel,
        out_shape=(*TABLES, jax.ShapeDtypeStruct((2 * PLACES, 128), F32)),
        in_specs=[VMEM] * 3,
        out_specs=[VMEM] * 5,
        scratch_shapes=[
            pltpu.VMEM((2 * PLACES * DEPTH, 128), F32),
            pltpu.VMEM((1, 9, DEPTH, 128), F32),
            pltpu.VMEM((6, 128, 128), F32),
        ],
        compiler_params=params(8),
        cost_estimate=pl.CostEstimate(
            flops=400_000_000, bytes_accessed=4_000_000, transcendentals=2_000_000
        ),
        name="early",
    )(left, fields, right)

    jump = jnp.where(slab == slabs - 1, SHEAR_JUMP, jnp.where(slab == 0, -SHEAR_JUMP, 0.0))
    density, accel = pl.pallas_call(
        late_kernel,
        out_shape=(
            jax.ShapeDtypeStruct((2, 8, 128), F32),
            jax.ShapeDtypeStruct((2, 3, 8, 128), F32),
        ),
        in_specs=[SMEM, SMEM] + [VMEM] * 7,
        out_specs=(VMEM, VMEM),
        scratch_shapes=[
            *scratch_of(TABLES, 4),
            pltpu.VMEM((4 * PLACES * DEPTH, 128), F32),
            pltpu.VMEM((2, 9, DEPTH, 128), F32),
            pltpu.VMEM((2 * PLACES, 128), F32),
            pltpu.VMEM((2 * PLACES, 128), F32),
            pltpu.VMEM((2 * PLACES * DEPTH, 128), F32),
            pltpu.VMEM((2 * PLACES * DEPTH, 128), F32),
            pltpu.VMEM((12, 128, 128), F32),
            pltpu.VMEM((2, 16 * 16, 128), F32),
        ],
        compiler_params=params(24),
        name="late",
    )(info, jump.astype(F32)[None], far, same, *tables)
    return (density, jnp.transpose(accel, (0, 2, 3, 1)))


def solution(mesh):
    placed = (
        P("gy", "gx", None, None),
        P("gy", "gx", None, None),
        P("gy", "gx", None),
        P("gy", "gx"),
        P(),
    )
    return jax.shard_map(
        functools.partial(local, "gy", "gx"),
        mesh=mesh,
        in_specs=placed,
        out_specs=(P("gy", "gx", None), P("gy", "gx", None, None)),
        check_vma=False,
    )
```

time: 81.5 us -> 64.5 us (0.79)
  the two profiles are of different devices: /device:TPU:7 before, /device:TPU:1 now
where the time goes in v2:
time: 64.5 us; the launch traced here: 64.1 us
  Pallas kernels  31.9 us (49%)
  starting transfers between devices  23.3 us (36%)
  waiting for transfers between devices  5.79 us (9%)
  local copies, waits for them, and re-layouts  1.63 us (3%)
  between operations  1.38 us (2%)
    pallas_call x1, Pallas kernels, local(): pl.pallas_call(late_kernel, out_shape=(jax.ShapeDtypeStruct((2, 8, 128),...  22.7 us
    ppermute x1, starting transfers between devices, local(): right = lax.ppermute(fields, columns_axis, [(j, i) for i, j in ring])  14.4 us
    pallas_call x1, Pallas kernels, local(): pl.pallas_call(early_kernel, out_shape=(*TABLES, jax.ShapeDtypeStruct((2...  6.5 us
    ppermute x1, waiting for transfers between devices, local(): left = lax.ppermute(fields, columns_axis, ring)  5.78 us
    ppermute x1, starting transfers between devices, local(): far = lax.ppermute(far, axes, far_pairs)  5.11 us
    pallas_call x1, Pallas kernels, local(): pl.pallas_call(pack_kernel, out_shape=jax.ShapeDtypeStruct((2, 7, 8, 128)...  2.09 us
    ppermute x1, starting transfers between devices, local(): same = lax.ppermute(same, axes, same_pairs)  1.92 us
    ppermute x1, starting transfers between devices, local(): left = lax.ppermute(fields, columns_axis, ring)  1.92 us
  transfers between devices with their start and end apart: 4, of which 1 were waited for; matrix products, arithmetic and copies ran while one was open for 0% of the time, Pallas kernels for 10%

profile of v2, /device:TPU:1, one launch (start us, length us, event | category | flops | bytes accessed | tf_op | source)
XLA Modules:
  0.0 64.1 jit_solution(1331720632384520591)
XLA Ops:
  0.6 2.1 %pack.1.own = f32[2,7,8,128]{3,2,1,0:T(8,128)} custom-call(s32[2,8]{1,0:T(2,128)} %counts.1, f32[2,3,8,128]{3,2,1,0:T(8,128)} %bitcast.7, f32[2,3,8,128]{3,2,1,0:T(8,128)} %bitcast.8, f32[2,8,128]{2,1,0:T(8,128)} %mass_hbm.1), custom_call_target="tpu_custom_call" | custom-call | tf_op jit(solution)/shard_map/pack/pallas_call | solution.py:420
  2.7 14.4 %collective-permute-start.1 = (f32[2,7,8,128]{3,2,1,0:T(8,128)}, f32[2,7,8,128]{3,2,1,0:T(8,128)S(1)}, u32[]{:S(2)}, u32[]{:S(2)}) collective-permute-start(f32[2,7,8,128]{3,2,1,0:T(8,128)} %pack.1.own), channel_id=1, source_target_pairs={{1,0},{2,1},{3,2},{4,3},{5,4},{6,5},{7,6},{8,7},{9,8},{10,9},{11,1... | collective-permute-start | bytes 172040 | tf_op jit(solution)/shard_map/ppermute | solution.py:440
  17.1 1.9 %collective-permute-start = (f32[2,7,8,128]{3,2,1,0:T(8,128)}, f32[2,7,8,128]{3,2,1,0:T(8,128)S(1)}, u32[]{:S(2)}, u32[]{:S(2)}) collective-permute-start(f32[2,7,8,128]{3,2,1,0:T(8,128)} %pack.1.own), channel_id=1, source_target_pairs={{0,1},{1,2},{2,3},{3,4},{4,5},{5,6},{6,7},{7,8},{8,9},{9,10},{10,1... | collective-permute-start | bytes 172040 | tf_op jit(solution)/shard_map/ppermute | solution.py:439
  19.7 0.1 pad_add_fusion.info
  19.8 0.0 collective-permute-done.1.right
  19.8 5.8 %collective-permute-done.left = f32[2,7,8,128]{3,2,1,0:T(8,128)S(1)} collective-permute-done((f32[2,7,8,128]{3,2,1,0:T(8,128)}, f32[2,7,8,128]{3,2,1,0:T(8,128)S(1)}, u32[]{:S(2)}, u32[]{:S(2)}) %collective-permute-start) | collective-permute-done | bytes 57376 | tf_op jit(solution)/shard_map/ppermute | solution.py:439
  25.6 0.0 copy-start
  25.6 0.8 %copy-done = f32[2,7,8,128]{3,2,1,0:T(8,128)S(1)} copy-done((f32[2,7,8,128]{3,2,1,0:T(8,128)S(1)}, f32[2,7,8,128]{3,2,1,0:T(8,128)}, u32[]{:S(2)}) %copy-start) | copy-done | bytes 57368
  26.4 0.6 window.1
  27.0 5.1 %collective-permute-start.2 = (f32[136,128]{1,0:T(8,128)S(1)}, f32[136,128]{1,0:T(8,128)S(1)}, u32[]{:S(2)}, u32[]{:S(2)}) collective-permute-start(f32[136,128]{1,0:T(8,128)S(1)} %get-tuple-element.11), channel_id=1, source_target_pairs={{0,480},{1,481},{2,482},{3,483},{4,484},{5,485},{6,486},{7,487},{8... | collective-permute-start | bytes 208904 | tf_op jit(solution)/shard_map/ppermute | solution.py:464
  32.1 1.9 %collective-permute-start.3 = (f32[136,128]{1,0:T(8,128)S(1)}, f32[136,128]{1,0:T(8,128)S(1)}, u32[]{:S(2)}, u32[]{:S(2)}) collective-permute-start(f32[136,128]{1,0:T(8,128)S(1)} %get-tuple-element.12), channel_id=1, source_target_pairs={{0,64},{1,65},{2,66},{3,67},{4,68},{5,69},{6,70},{7,71},{8,72},{9,... | collective-permute-start | bytes 208904 | tf_op jit(solution)/shard_map/ppermute | solution.py:465
  34.0 0.0 copy-start.1
  34.0 0.8 %copy-done.1 = f32[2,7,8,128]{3,2,1,0:T(8,128)S(1)} copy-done((f32[2,7,8,128]{3,2,1,0:T(8,128)S(1)}, f32[2,7,8,128]{3,2,1,0:T(8,128)}, u32[]{:S(2)}) %copy-start.1) | copy-done | bytes 57368
  34.9 6.5 %early.1 = (f32[2,7,16,128]{3,2,1,0:T(8,128)S(1)}, f32[1024,128]{1,0:T(8,128)S(1)}, bf16[32,128,32]{2,1,0:T(8,128)(2,1)S(1)}, f32[32,128,128]{2,1,0:T(8,128)S(1)}, f32[32,128]{1,0:T(8,128)S(1)}) custom-call(f32[2,7,8,128]{3,2,1,0:T(8,128)S(1)} %collective-permute-done.left, f32[2,7,8,128]{3,2,1,0:T(8,128)S(1)} %copy-done.1, ...), custom_call_target="tpu_custom_call" | custom-call | flops 400000000 | bytes 4000000 | tf_op jit(solution)/shard_map/early/pallas_call | solution.py:467
  41.4 0.0 collective-permute-done.2.far
  41.4 0.0 collective-permute-done.3.same
  41.4 22.7 %late.1 = (f32[2,8,128]{2,1,0:T(8,128)}, f32[2,3,8,128]{3,2,1,0:T(8,128)}) custom-call(s32[2]{0:T(128)S(1)} %pad_add_fusion.info, f32[1]{0:T(128)} %bitcast.3.jump_ref, f32[136,128]{1,0:T(8,128)S(1)} %collective-permute-done.2.far, f32[136,128]{1,0:T(8,128)S(1)} %collective-permute-done.3.same, f32[2,7,16,128]{3,2,1,0:T(8,128)S(1)} %get-tuple-element.13.fields, ...), custom_call_target="tpu_custom_call" | custom-call | tf_op jit(solution)/shard_map/late/pallas_call | solution.py:485
Async XLA Ops:
  2.7 17.1 %collective-permute-start.1 = (f32[2,7,8,128]{3,2,1,0:T(8,128)}, f32[2,7,8,128]{3,2,1,0:T(8,128)S(1)}, u32[]{:S(2)}, u32[]{:S(2)}) collective-permute-start(f32[2,7,8,128]{3,2,1,0:T(8,128)} %pack.1.own), channel_id=1, source_target_pairs={{1,0},{2,1},{3,2},{4,3},{5,4},{6,5},{7,6},{8,7},{9,8},{10,9},{11,1... | collective-permute-start | bytes 172040 | tf_op jit(solution)/shard_map/ppermute | solution.py:440
  17.1 8.5 %collective-permute-start = (f32[2,7,8,128]{3,2,1,0:T(8,128)}, f32[2,7,8,128]{3,2,1,0:T(8,128)S(1)}, u32[]{:S(2)}, u32[]{:S(2)}) collective-permute-start(f32[2,7,8,128]{3,2,1,0:T(8,128)} %pack.1.own), channel_id=1, source_target_pairs={{0,1},{1,2},{2,3},{3,4},{4,5},{5,6},{6,7},{7,8},{8,9},{9,10},{10,1... | collective-permute-start | bytes 172040 | tf_op jit(solution)/shard_map/ppermute | solution.py:439
  25.6 0.8 %copy-start = (f32[2,7,8,128]{3,2,1,0:T(8,128)S(1)}, f32[2,7,8,128]{3,2,1,0:T(8,128)}, u32[]{:S(2)}) copy-start(f32[2,7,8,128]{3,2,1,0:T(8,128)} %pack.1.own) | copy-start | bytes 172036
  27.0 14.4 %collective-permute-start.2 = (f32[136,128]{1,0:T(8,128)S(1)}, f32[136,128]{1,0:T(8,128)S(1)}, u32[]{:S(2)}, u32[]{:S(2)}) collective-permute-start(f32[136,128]{1,0:T(8,128)S(1)} %get-tuple-element.11), channel_id=1, source_target_pairs={{0,480},{1,481},{2,482},{3,483},{4,484},{5,485},{6,486},{7,487},{8... | collective-permute-start | bytes 208904 | tf_op jit(solution)/shard_map/ppermute | solution.py:464
  32.1 9.3 %collective-permute-start.3 = (f32[136,128]{1,0:T(8,128)S(1)}, f32[136,128]{1,0:T(8,128)S(1)}, u32[]{:S(2)}, u32[]{:S(2)}) collective-permute-start(f32[136,128]{1,0:T(8,128)S(1)} %get-tuple-element.12), channel_id=1, source_target_pairs={{0,64},{1,65},{2,66},{3,67},{4,68},{5,69},{6,70},{7,71},{8,72},{9,... | collective-permute-start | bytes 208904 | tf_op jit(solution)/shard_map/ppermute | solution.py:465
  34.0 0.8 %copy-start.1 = (f32[2,7,8,128]{3,2,1,0:T(8,128)S(1)}, f32[2,7,8,128]{3,2,1,0:T(8,128)}, u32[]{:S(2)}) copy-start(f32[2,7,8,128]{3,2,1,0:T(8,128)} %pack.1.own) | copy-start | bytes 172036

commit v3 on v2

--- a/solution.py
+++ b/solution.py
@@ -1,4 +1,3 @@
-import functools
 import math
 
 import jax
@@ -8,6 +7,7 @@
 from jax.experimental.pallas import tpu as pltpu
 from jax.sharding import PartitionSpec as P
 
+
 SMOOTHING = 0.5
 KERNEL_NORM = 1.0 / (math.pi * SMOOTHING**3)
 SOUND_SQ = 0.2
@@ -17,42 +17,22 @@
 
 COLS, PLACES = 12, 16
 DEPTH = 32
-NEAR, FAR = 7, 4
+NEAR = 7
 SENT = 136
 BF16, F32 = jnp.bfloat16, jnp.float32
 NEIGHBOURS = [(a, b) for a in (-1, 0, 1) for b in (-1, 0, 1)]
 VMEM = pl.BlockSpec(memory_space=pltpu.VMEM)
 SMEM = pl.BlockSpec(memory_space=pltpu.SMEM)
-HBM = pl.BlockSpec(memory_space=pltpu.HBM)
 TABLES = (
     jax.ShapeDtypeStruct((2, 7, PLACES, 128), F32),
     jax.ShapeDtypeStruct((2 * PLACES * DEPTH, 128), F32),
-    jax.ShapeDtypeStruct((2 * PLACES, 128, DEPTH), BF16),
-    jax.ShapeDtypeStruct((2 * PLACES, 128, 128), F32),
+    jax.ShapeDtypeStruct((2 * COLS, 128, DEPTH), BF16),
+    jax.ShapeDtypeStruct((2 * COLS, 128, 128), F32),
 )
 
 
-def pack_kernel(counts, pos_hbm, vel_hbm, mass_hbm, out, pos, vel, mass, sems):
-    copies = [
-        pltpu.make_async_copy(source, to, sems.at[n])
-        for n, (source, to) in enumerate(((pos_hbm, pos), (vel_hbm, vel), (mass_hbm, mass)))
-    ]
-    for copy in copies:
-        copy.start()
-    slot = lax.broadcasted_iota(jnp.int32, (8, 128), 1)
-    column = lax.broadcasted_iota(jnp.int32, (8, 128), 0)
-    limits = []
-    for row in range(2):
-        limit = jnp.zeros((8, 128), jnp.int32)
-        for c in range(8):
-            limit = jnp.where(column == c, counts[row, c], limit)
-        limits.append(limit)
-    for copy in copies:
-        copy.wait()
-    for row in range(2):
-        out[row, 0:3] = pos[row]
-        out[row, 3:6] = vel[row]
-        out[row, 6] = jnp.where(slot < limits[row], mass[row], 0.0)
+def place_of(column):
+    return jnp.where(column < 0, column + 10, jnp.where(column > 7, column + 2, column))
 
 
 def window_kernel(info, left, own, right, far_out, same_out):
@@ -98,15 +78,18 @@
             scales[1, n] = scale
 
 
-def build_tables(rows, fields, irows, jcols, masses, jrows):
+def build_tables(rows, halves, fields, irows, jcols, masses, jrows):
     k = lax.broadcasted_iota(jnp.int32, (DEPTH, 128), 0)
     ones_j = jnp.where(((k >= 15) & (k < 20)) | (k == 22) | (k == 23) | (k == 26), 1.0, 0.0)
     ones_i = jnp.where((k >= 12) & (k < 15), 1.0, 0.0)
     ones_i = jnp.where((k == 20) | (k == 21) | (k >= 24) & (k < 27), 4.0, ones_i)
     pick_mass = jnp.where((k >= 27) & (k < 30), 1.0, 0.0).astype(BF16)
 
-    def build(step, carry):
-        row, half = step // 2, step % 2
+    count = len(halves)
+
+    def build(n, carry):
+        row, half = n // count, n % count + halves[0]
+        step = row * 2 + half
         base = pl.multiple_of(step * (8 * DEPTH), 8 * DEPTH)
         cells = pl.ds(pl.multiple_of(half * 8, 8), 8)
         for c in range(8):
@@ -138,18 +121,22 @@
             put(jrows, 27 + k, part)
         return carry
 
-    lax.fori_loop(0, rows * 2, build, 0)
+    lax.fori_loop(0, rows * count, build, 0)
 
     def turn_row(row, carry):
-        for c in range(COLS):
+        for c in range(8 * halves[0], 8 if halves[-1] == 0 else COLS):
             cell = row * PLACES + c
             table = jrows[pl.ds(pl.multiple_of(cell * DEPTH, DEPTH), DEPTH), :]
             flipped = table.T.astype(BF16)
-            jcols[cell] = flipped
-            masses[cell] = jnp.dot(flipped, pick_mass, preferred_element_type=F32)
+            jcols[row * COLS + c] = flipped
+            masses[row * COLS + c] = jnp.dot(flipped, pick_mass, preferred_element_type=F32)
         return carry
 
     lax.fori_loop(0, rows, turn_row, 0)
+
+
+def packed(cell):
+    return cell - (PLACES - COLS) * (cell // PLACES)
 
 
 def rows_of(table, cell):
@@ -162,6 +149,7 @@
 
 
 def add_density(total, dist, m, masses, cell):
+    cell = packed(cell)
     for at in range(0, 128, 32):
         y = jnp.maximum(dist[m, at : at + 32, :], 1e-12)
         q = y * lax.rsqrt(y)
@@ -181,50 +169,105 @@
     return direction * 3 + b + 1
 
 
-def early_kernel(left, own, right, fields, irows, jcols, masses, rhos, jrows, scales, dist):
-    fields[...] = jnp.zeros_like(fields)
-    for row in range(2):
-        for f in range(7):
-            fields[row, f, 0:2, :] = left[row, f, 6:8, :]
-            fields[row, f, 2:10, :] = own[row, f]
-            fields[row, f, 10:12, :] = right[row, f, 0:2, :]
-    fill_scales(scales)
-    build_tables(2, fields, irows, jcols, masses, jrows)
-
-    def blocks(n):
-        side, column = n // 10, n % 10 + 1
-        cell = side * PLACES + column
-        other = (1 - side) * PLACES + column
-        return cell, [
-            (row_index(direction, b), at + b)
-            for direction, at in ((1, cell), (2 - 2 * side, other))
-            for b in (-1, 0, 1)
-        ]
-
-    def measure(n, m):
-        cell, near = blocks(n)
-        put_distances(dist, m, rows_of(irows, cell), scales[0, near[m][0]], jcols[near[m][1]])
-
-    def step(n, carry):
-        cell, near = blocks(n)
-        following = jnp.minimum(n + 1, 19)
-        total = jnp.zeros((8, 128), F32)
+def own_kernel(run, own, *refs):
+    fields, irows, jcols, masses, rhos, jrows, scales, dist = refs[-8:]
+
+    @pl.when(run[0] == 1)
+    def _():
+        fields[...] = jnp.zeros_like(fields)
+        for row in range(2):
+            for f in range(7):
+                fields[row, f, 0:8, :] = own[row, f]
+        fill_scales(scales)
+        build_tables(2, (0,), fields, irows, jcols, masses, jrows)
+        jcols[8] = jnp.zeros((128, DEPTH), BF16)
+        masses[8] = jnp.zeros((128, 128), F32)
+
+        def blocks(n):
+            side, column = n // 8, n % 8
+            found = []
+            for direction, row in ((1, side), (2 - 2 * side, 1 - side)):
+                for b in (-1, 0, 1):
+                    at = column + b
+                    inside = (at >= 0) & (at < 8)
+                    found.append(
+                        (row_index(direction, b), jnp.where(inside, row * PLACES + at, 8))
+                    )
+            return side * PLACES + column, found
+
+        def measure(n, m):
+            cell, near = blocks(n)
+            columns = jcols[packed(near[m][1])]
+            put_distances(dist, m, rows_of(irows, cell), scales[0, near[m][0]], columns)
+
+        def step(n, carry):
+            cell, near = blocks(n)
+            following = jnp.minimum(n + 1, 15)
+            total = jnp.zeros((8, 128), F32)
+            for m in range(6):
+                total = add_density(total, dist, m, masses, near[m][1])
+                measure(following, m)
+            rhos[pl.ds(cell, 1), :] = density_of(total)
+            return carry
+
+        rhos[...] = jnp.zeros_like(rhos)
         for m in range(6):
-            total = add_density(total, dist, m, masses, near[m][1])
-            measure(following, m)
-        rhos[pl.ds(cell, 1), :] = density_of(total)
-        return carry
-
-    rhos[...] = jnp.zeros_like(rhos)
-    for m in range(6):
-        measure(0, m)
-    lax.fori_loop(0, 20, step, 0)
+            measure(0, m)
+        lax.fori_loop(0, 16, step, 0)
+
+
+def beside_kernel(run, left, right, *refs):
+    fields, irows, jcols, masses, rhos, jrows, scales, dist = refs[-8:]
+
+    @pl.when(run[0] == 1)
+    def _():
+        for row in range(2):
+            for f in range(7):
+                fields[row, f, 8:10, :] = left[row, f, 6:8, :]
+                fields[row, f, 10:12, :] = right[row, f, 0:2, :]
+        fill_scales(scales)
+        build_tables(2, (1,), fields, irows, jcols, masses, jrows)
+
+        def blocks(n):
+            side, far = n // 2, n % 2
+            outer, inner = jnp.where(far == 1, 8, -1), jnp.where(far == 1, 7, 0)
+            found = []
+            for direction, row in ((1, side), (2 - 2 * side, 1 - side)):
+                for b in (-1, 0, 1):
+                    at = row * PLACES + place_of(outer + b)
+                    found.append((0, row_index(direction, b), at))
+                at = row * PLACES + place_of(outer)
+                found.append((1, row_index(direction, 2 * far - 1), at))
+            cells = [side * PLACES + place_of(column) for column in (outer, inner)]
+            return cells, found
+
+        def measure(n, m):
+            cells, near = blocks(n)
+            which, index, at = near[m]
+            table = rows_of(irows, cells[which])
+            put_distances(dist, m, table, scales[0, index], jcols[packed(at)])
+
+        def step(n, carry):
+            cells, near = blocks(n)
+            following = jnp.minimum(n + 1, 3)
+            totals = [jnp.zeros((8, 128), F32)] * 2
+            for m in range(8):
+                which, _, at = near[m]
+                totals[which] = add_density(totals[which], dist, m, masses, at)
+                measure(following, m)
+            rhos[pl.ds(cells[0], 1), :] = density_of(totals[0])
+            rhos[pl.ds(cells[1], 1), :] = density_of(totals[1]) + rhos[pl.ds(cells[1], 1), :]
+            return carry
+
+        for m in range(8):
+            measure(0, m)
+        lax.fori_loop(0, 4, step, 0)
 
 
 def late_kernel(
     info, jump_ref, far, same, fields, irows, jcols, masses, partial, density, accel,
     ghosts, ghost_irows, ghost_jcols, ghost_masses, jrows,
-    scales, rhos, ghost_rhos, crows, ghost_crows, dist, sums,
+    scales, rhos, ghost_rhos, crows, ghost_crows, dist, sums, even_slopes, odd_slopes,
 ):
     odd, jump = info[0], jump_ref[0]
 
@@ -234,41 +277,45 @@
             value = piece[f * COLS : (f + 1) * COLS, :]
             if piece is far and f == 3:
                 value = value + jump
-            ghosts[side, f, 0:COLS, :] = value
+            ghosts[side, f, 0:8, :] = value[2:10]
+            ghosts[side, f, 8:10, :] = value[0:2]
+            ghosts[side, f, 10:12, :] = value[10:12]
         for n, f in enumerate((0, 1, 2, 6)):
             at = (NEAR + n) * COLS
-            ghosts[2 + side, f, 0:COLS, :] = piece[at : at + COLS, :]
+            value = piece[at : at + COLS, :]
+            ghosts[2 + side, f, 0:8, :] = value[2:10]
+            ghosts[2 + side, f, 8:10, :] = value[0:2]
+            ghosts[2 + side, f, 10:12, :] = value[10:12]
     fill_scales(scales)
-    build_tables(4, ghosts, ghost_irows, ghost_jcols, ghost_masses, jrows)
+    build_tables(4, (0, 1), ghosts, ghost_irows, ghost_jcols, ghost_masses, jrows)
 
     def blocks(n):
-        side, column = n // 10, n % 10 + 1
-        cell = side * PLACES + column
-        return cell, side, [
-            (who, row_index(direction, b), at + b)
-            for who, direction, at in (
-                ("far", 2 * side, cell + 2 * PLACES),
-                ("near", 1, cell),
-                ("own", 2 - 2 * side, cell),
-                ("mine", 2 * side, cell),
+        side, column = n // 10, n % 10 - 1
+        return side * PLACES + place_of(column), side, [
+            (who, row_index(direction, b), row * PLACES + place_of(column + b))
+            for who, direction, row in (
+                ("far", 2 * side, side + 2),
+                ("near", 1, side),
+                ("own", 2 - 2 * side, side),
+                ("mine", 2 * side, side),
             )
             for b in (-1, 0, 1)
         ]
 
     def measure(n, m):
-        cell, side, near = blocks(n)
+        cell, _, near = blocks(n)
         who, index, at = near[m]
         table = rows_of(irows if who == "mine" else ghost_irows, cell)
-        columns = (jcols if who == "own" else ghost_jcols)[at]
+        columns = (jcols if who == "own" else ghost_jcols)[packed(at)]
         put_distances(dist, m, table, scales[0, index], columns)
 
     def density_step(n, carry):
-        cell, side, near = blocks(n)
+        cell, _, near = blocks(n)
         following = jnp.minimum(n + 1, 19)
         ghost_total = jnp.zeros((8, 128), F32)
         own_total = jnp.zeros((8, 128), F32)
         for m in range(12):
-            who, index, at = near[m]
+            who, _, at = near[m]
             which = masses if who == "own" else ghost_masses
             if who == "mine":
                 own_total = add_density(own_total, dist, m, which, at)
@@ -316,15 +363,13 @@
     coefficients(ghosts, ghost_rhos, ghost_crows)
 
     def force_blocks(n):
-        side, column = n // 8, n % 8 + 2
-        cell = side * PLACES + column
-        other = (1 - side) * PLACES + column
-        return cell, [
-            (ghost, row_index(direction, b), at + b)
-            for ghost, direction, at in (
-                (True, 2 * side, cell),
-                (False, 1, cell),
-                (False, 2 - 2 * side, other),
+        side, column = n // 8, n % 8
+        return side * PLACES + column, [
+            (ghost, row_index(direction, b), row * PLACES + place_of(column + b))
+            for ghost, direction, row in (
+                (True, 2 * side, side),
+                (False, 1, side),
+                (False, 2 - 2 * side, 1 - side),
             )
             for b in (-1, 0, 1)
         ]
@@ -332,18 +377,29 @@
     def force_measure(n, m):
         cell, near = force_blocks(n)
         ghost, index, at = near[m]
-        columns = (ghost_jcols if ghost else jcols)[at]
+        columns = (ghost_jcols if ghost else jcols)[packed(at)]
         put_distances(dist, m, rows_of(irows, cell), scales[0, index], columns)
 
-    def force_step(n, carry):
-        cell, near = force_blocks(n)
-        following = jnp.minimum(n + 1, 15)
+    def gather_sums(n, slopes):
+        _, near = force_blocks(n)
         total = jnp.zeros((DEPTH, 256), F32)
         for m in range(9):
             ghost, index, at = near[m]
             table = rows_of(ghost_crows if ghost else crows, at)
             left_side = (table * scales[1, index]).astype(BF16)
-            highs, lows = [], []
+            total = total + jnp.dot(
+                jnp.concatenate([left_side, left_side], axis=1),
+                slopes[256 * m : 256 * (m + 1), :],
+                preferred_element_type=F32,
+            )
+        total = total[0:16] + total[16:32]
+        for half in range(2):
+            at = pl.ds(pl.multiple_of(n * 16, 16), 16)
+            sums[half, at, :] = total[:, 128 * half : 128 * (half + 1)]
+
+    def put_slopes(n, slopes):
+        following = jnp.minimum(n + 1, 15)
+        for m in range(9):
             for at in range(0, 128, 32):
                 y = jnp.maximum(dist[m, at : at + 32, :], 1e-12)
                 inverse = lax.rsqrt(y)
@@ -354,29 +410,27 @@
                 damped = slope * (y * (soft * soft))
                 both = jnp.concatenate([slope, damped], axis=1)
                 high = both.astype(BF16)
-                highs.append(high)
-                lows.append((both - high.astype(F32)).astype(BF16))
+                base = 256 * m + at
+                slopes[base : base + 32, :] = high
+                slopes[base + 128 : base + 160, :] = (both - high.astype(F32)).astype(BF16)
             force_measure(following, m)
-            total = total + jnp.dot(
-                left_side, jnp.concatenate(highs, axis=0), preferred_element_type=F32
-            )
-            total = total + jnp.dot(
-                left_side, jnp.concatenate(lows, axis=0), preferred_element_type=F32
-            )
-        total = total[0:16] + total[16:32]
-        for half in range(2):
-            at = pl.ds(pl.multiple_of(n * 16, 16), 16)
-            sums[half, at, :] = total[:, 128 * half : 128 * (half + 1)]
+
+    def force_step(n, carry):
+        gather_sums(jnp.maximum(2 * n - 1, 0), odd_slopes)
+        put_slopes(2 * n, even_slopes)
+        gather_sums(2 * n, even_slopes)
+        put_slopes(2 * n + 1, odd_slopes)
         return carry
 
     for m in range(9):
         force_measure(0, m)
-    lax.fori_loop(0, 16, force_step, 0)
+    lax.fori_loop(0, 8, force_step, 0)
+    gather_sums(15, odd_slopes)
 
     for row in range(2):
-        mass = fields[row, 6, 2:10, :]
+        mass = fields[row, 6, 0:8, :]
         valid = mass > 0.0
-        rho = rhos[row * PLACES + 2 : row * PLACES + 10, :]
+        rho = rhos[row * PLACES : row * PLACES + 8, :]
         density[row] = jnp.where(valid, rho, 0.0)
         inverse_rho = 1.0 / jnp.where(valid, rho, 1.0)
 
@@ -387,14 +441,14 @@
         pressure_scale = -3.0 * KERNEL_NORM * -SOUND_SQ * 0.5
         viscous_scale = -3.0 * KERNEL_NORM * 2.0 * VISCOSITY
         for f in range(3):
-            high, low = parts_of(2.0 * fields[row, f, 2:10, :] - 1.0, 2)
+            high, low = parts_of(2.0 * fields[row, f, 0:8, :] - 1.0, 2)
             x = high + low
             first = x * mass_sum - term(1 + f, 0)
             second = x * share_sum - term(7 + f, 0)
             if f < 2:
                 first = first - 2.0 * term(4 + f, 0)
                 second = second - 2.0 * term(10 + f, 0)
-            viscous = fields[row, 3 + f, 2:10, :] * drag_sum - term(12 + f, 1)
+            viscous = fields[row, 3 + f, 0:8, :] * drag_sum - term(12 + f, 1)
             value = pressure_scale * (first * inverse_rho + second)
             value = value + viscous_scale * viscous * inverse_rho
             accel[row, f] = jnp.where(valid, value, 0.0)
@@ -417,27 +471,54 @@
     slab = lax.axis_index(rows_axis)
     past = shear_shift[0] - half * particle_mass.shape[1]
 
-    fields = pl.pallas_call(
-        pack_kernel,
-        out_shape=jax.ShapeDtypeStruct((2, 7, 8, 128), F32),
-        in_specs=[SMEM, HBM, HBM, HBM],
-        out_specs=VMEM,
-        scratch_shapes=[
-            pltpu.VMEM((2, 3, 8, 128), F32),
-            pltpu.VMEM((2, 3, 8, 128), F32),
-            pltpu.VMEM((2, 8, 128), F32),
-            pltpu.SemaphoreType.DMA((3,)),
+    slot = jnp.arange(particle_mass.shape[2], dtype=jnp.int32)
+    weight = jnp.where(slot < cell_counts[:, :, None], particle_mass, 0.0)
+    ring = [(i, (i + 1) % blocks) for i in range(blocks)]
+    fields = jnp.concatenate(
+        [
+            jnp.transpose(position, (0, 3, 1, 2)),
+            jnp.transpose(velocity, (0, 3, 1, 2)),
+            weight[:, None],
         ],
-        name="pack",
-    )(
-        cell_counts,
-        jnp.transpose(position, (0, 3, 1, 2)),
-        jnp.transpose(velocity, (0, 3, 1, 2)),
-        particle_mass,
+        axis=1,
     )
-    ring = [(i, (i + 1) % blocks) for i in range(blocks)]
+    shapes = (*TABLES, jax.ShapeDtypeStruct((2 * PLACES, 128), F32))
+
+    def tables_call(kernel, run, inputs, tables, blocks):
+        count = len(inputs) + 1
+        return pl.pallas_call(
+            kernel,
+            out_shape=shapes,
+            in_specs=[SMEM] + [VMEM] * (len(inputs) + len(tables)),
+            out_specs=[VMEM] * 5,
+            scratch_shapes=[
+                pltpu.VMEM((2 * PLACES * DEPTH, 128), F32),
+                pltpu.VMEM((1, 9, DEPTH, 128), F32),
+                pltpu.VMEM((blocks, 128, 128), F32),
+            ],
+            input_output_aliases={count + n: n for n in range(len(tables))},
+            compiler_params=params(8),
+            cost_estimate=pl.CostEstimate(
+                flops=100_000_000, bytes_accessed=4_000_000, transcendentals=1_000_000
+            ),
+        )(run.astype(jnp.int32)[None], *inputs, *tables)
+
+    block = lax.axis_index(columns_axis)
+    edge = (slab == 0) | (slab == slabs - 1)
+    own_now = [block <= 1, (block > 1) & ~(edge & (block >= half)), edge & (block >= half)]
+    soon = edge & (block > 1) & (block < half)
+    beside_now = [soon, ~edge, edge & ~soon]
+
+    def own_work(which, tables):
+        return tables_call(own_kernel, own_now[which], (fields,), tables, 6)
+
+    def beside_work(which, tables):
+        return tables_call(beside_kernel, beside_now[which], (left, right), tables, 8)
+
     left = lax.ppermute(fields, columns_axis, ring)
+    tables = own_work(0, ())
     right = lax.ppermute(fields, columns_axis, [(j, i) for i, j in ring])
+    tables = own_work(1, tables)
 
     odd = lax.rem(slab, 2)
     start = 6 + jnp.where(slab == slabs - 1, past, jnp.where(slab == 0, -past, 0))
@@ -461,25 +542,12 @@
             if other < 0 or other >= slabs:
                 other, to = other % slabs, (b + half) % blocks
             far_pairs.append((me, other * blocks + to))
+    tables = beside_work(0, tables)
     far = lax.ppermute(far, axes, far_pairs)
+    tables = beside_work(1, tables)
     same = lax.ppermute(same, axes, same_pairs)
-
-    tables = pl.pallas_call(
-        early_kernel,
-        out_shape=(*TABLES, jax.ShapeDtypeStruct((2 * PLACES, 128), F32)),
-        in_specs=[VMEM] * 3,
-        out_specs=[VMEM] * 5,
-        scratch_shapes=[
-            pltpu.VMEM((2 * PLACES * DEPTH, 128), F32),
-            pltpu.VMEM((1, 9, DEPTH, 128), F32),
-            pltpu.VMEM((6, 128, 128), F32),
-        ],
-        compiler_params=params(8),
-        cost_estimate=pl.CostEstimate(
-            flops=400_000_000, bytes_accessed=4_000_000, transcendentals=2_000_000
-        ),
-        name="early",
-    )(left, fields, right)
+    tables = own_work(2, tables)
+    tables = beside_work(2, tables)
 
     jump = jnp.where(slab == slabs - 1, SHEAR_JUMP, jnp.where(slab == 0, -SHEAR_JUMP, 0.0))
     density, accel = pl.pallas_call(
@@ -500,6 +568,8 @@
             pltpu.VMEM((2 * PLACES * DEPTH, 128), F32),
             pltpu.VMEM((12, 128, 128), F32),
             pltpu.VMEM((2, 16 * 16, 128), F32),
+            pltpu.VMEM((9 * 256, 256), BF16),
+            pltpu.VMEM((9 * 256, 256), BF16),
         ],
         compiler_params=params(24),
         name="late",
@@ -515,8 +585,12 @@
         P("gy", "gx"),
         P(),
     )
+
+    def step(*args):
+        return local("gy", "gx", *args)
+
     return jax.shard_map(
-        functools.partial(local, "gy", "gx"),
+        step,
         mesh=mesh,
         in_specs=placed,
         out_specs=(P("gy", "gx", None), P("gy", "gx", None, None)),

time: 64.5 us -> 58.9 us (0.913)
  waiting for transfers between devices: 5.79 us -> 0.5 us
  local copies, waits for them, and re-layouts: 1.63 us -> 0 us
  other arithmetic: 0.08 us -> 1.61 us
  Pallas kernels: 31.9 us -> 30.5 us
  starting transfers between devices: 23.3 us -> 24.5 us
    ppermute x1, waiting for transfers between devices: 5.78 us -> 0.01 us  [local(): left = lax.ppermute(fields, columns_axis, ring)]
    ppermute x1, starting transfers between devices: 14.4 us -> 12.3 us  [local(): right = lax.ppermute(fields, columns_axis, [(j, i) for i, j in ring])]
    ppermute x1, starting transfers between devices: 1.92 us -> 4.01 us  [local(): left = lax.ppermute(fields, columns_axis, ring)]
    ppermute x1, starting transfers between devices: 1.92 us -> 3.71 us  [local(): same = lax.ppermute(same, axes, same_pairs)]
    unnamed x4 -> x0, local copies, waits for them, and re-layouts: 1.63 us -> none
    pallas_call x2 -> x6, Pallas kernels: 8.59 us -> 7.7 us  [tables_call(): pl.pallas_call(kernel, out_shape=shapes, in_specs=[SMEM] + [VMEM] * (len(...]
    broadcast_in_dim x0 -> x1, other arithmetic: none -> 0.77 us  [local(): weight[:, None]]
    concatenate x0 -> x1, other arithmetic: none -> 0.76 us  [local(): jnp.concatenate([jnp.transpose(position, (0, 3, 1, 2)), jnp.transpose(vel...]
  transfers between devices with their start and end apart: 4 -> 4, of which waited for: 1 -> 1; matrix products, arithmetic and copies ran while one was open for 0% -> 0% of each run, Pallas kernels for 10% -> 13%
where the time goes in v3:
time: 58.9 us; the launch traced here: 58.6 us
  Pallas kernels  30.5 us (52%)
  starting transfers between devices  24.5 us (42%)
  other arithmetic  1.61 us (3%)
  between operations  1.43 us (2%)
    pallas_call x1, Pallas kernels, local(): pl.pallas_call(late_kernel, out_shape=(jax.ShapeDtypeStruct((2, 8, 128),...  22.3 us
    ppermute x1, starting transfers between devices, local(): right = lax.ppermute(fields, columns_axis, [(j, i) for i, j in ring])  12.3 us
    pallas_call x6, Pallas kernels, tables_call(): pl.pallas_call(kernel, out_shape=shapes, in_specs=[SMEM] + [VMEM] * (len(...  7.7 us
    ppermute x1, starting transfers between devices, local(): far = lax.ppermute(far, axes, far_pairs)  4.53 us
    ppermute x1, starting transfers between devices, local(): left = lax.ppermute(fields, columns_axis, ring)  4.01 us
    ppermute x1, starting transfers between devices, local(): same = lax.ppermute(same, axes, same_pairs)  3.71 us
  transfers between devices with their start and end apart: 4, of which 1 were waited for; matrix products, arithmetic and copies ran while one was open for 0% of the time, Pallas kernels for 13%

profile of v3, /device:TPU:1, one launch (start us, length us, event | category | flops | bytes accessed | tf_op | source)
XLA Modules:
  0.0 58.6 jit_solution(2917392811380026291)
XLA Ops:
  0.6 0.8 %select_bitcast_fusion = f32[2,1,8,128]{3,2,1,0:T(8,128)S(1)} fusion(f32[2,8,128]{2,1,0:T(8,128)} %param.7, s32[2,8]{1,0:T(2,128)} %param.8), kind=kLoop, calls=%fused_computation.1 | loop fusion | flops 4096 | bytes 16448 | tf_op jit(solution)/shard_map/broadcast_in_dim | solution.py:481
  1.4 0.8 %pad_maximum_fusion.own = f32[2,7,8,128]{3,2,1,0:T(8,128)S(1)} fusion(f32[2,1,8,128]{3,2,1,0:T(8,128)S(1)} %select_bitcast_fusion, f32[2,3,8,128]{3,2,1,0:T(8,128)} %bitcast.15, f32[2,3,8,128]{3,2,1,0:T(8,128)} %bitcast.16), kind=kLoop, calls=%fused_computation | loop fusion | flops 28672 | bytes 114688 | tf_op jit(solution)/shard_map/concatenate | solution.py:477
  2.2 4.0 %collective-permute-start = (f32[2,7,8,128]{3,2,1,0:T(8,128)S(1)}, f32[2,7,8,128]{3,2,1,0:T(8,128)S(1)}, u32[]{:S(2)}, u32[]{:S(2)}) collective-permute-start(f32[2,7,8,128]{3,2,1,0:T(8,128)S(1)} %pad_maximum_fusion.own), channel_id=1, source_target_pairs={{0,1},{1,2},{2,3},{3,4},{4,5},{5,6},{6,7},{7,8},{8,9},{9,10},{10,1... | collective-permute-start | bytes 172040 | tf_op jit(solution)/shard_map/ppermute | solution.py:518
  6.2 12.3 %collective-permute-start.1 = (f32[2,7,8,128]{3,2,1,0:T(8,128)S(1)}, f32[2,7,8,128]{3,2,1,0:T(8,128)S(1)}, u32[]{:S(2)}, u32[]{:S(2)}) collective-permute-start(f32[2,7,8,128]{3,2,1,0:T(8,128)S(1)} %pad_maximum_fusion.own), channel_id=1, source_target_pairs={{1,0},{2,1},{3,2},{4,3},{5,4},{6,5},{7,6},{8,7},{9,8},{10,9},{11,1... | collective-permute-start | bytes 172040 | tf_op jit(solution)/shard_map/ppermute | solution.py:520
  19.1 0.1 pad_add_fusion.info
  19.2 0.0 collective-permute-done.left
  19.2 0.5 collective-permute-done.1.right
  19.7 0.6 window.1
  20.3 4.5 %collective-permute-start.2 = (f32[136,128]{1,0:T(8,128)S(1)}, f32[136,128]{1,0:T(8,128)S(1)}, u32[]{:S(2)}, u32[]{:S(2)}) collective-permute-start(f32[136,128]{1,0:T(8,128)S(1)} %get-tuple-element.36), channel_id=1, source_target_pairs={{0,480},{1,481},{2,482},{3,483},{4,484},{5,485},{6,486},{7,487},{8... | collective-permute-start | bytes 208904 | tf_op jit(solution)/shard_map/ppermute | solution.py:546
  24.8 3.7 %collective-permute-start.3 = (f32[136,128]{1,0:T(8,128)S(1)}, f32[136,128]{1,0:T(8,128)S(1)}, u32[]{:S(2)}, u32[]{:S(2)}) collective-permute-start(f32[136,128]{1,0:T(8,128)S(1)} %get-tuple-element.37), channel_id=1, source_target_pairs={{0,64},{1,65},{2,66},{3,67},{4,68},{5,69},{6,70},{7,71},{8,72},{9,... | collective-permute-start | bytes 208904 | tf_op jit(solution)/shard_map/ppermute | solution.py:548
  28.6 5.4 %shard_map.68 = (f32[2,7,16,128]{3,2,1,0:T(8,128)S(1)}, f32[1024,128]{1,0:T(8,128)S(1)}, bf16[24,128,32]{2,1,0:T(8,128)(2,1)S(1)}, f32[24,128,128]{2,1,0:T(8,128)S(1)}, f32[32,128]{1,0:T(8,128)S(1)}) custom-call(s32[1]{0:T(128)} %bitcast.12.run, f32[2,7,8,128]{3,2,1,0:T(8,128)S(1)} %pad_maximum_fusion.own), custom_call_target="tpu_custom_call" | custom-call | flops 100000000 | bytes 4000000 | tf_op jit(solution)/shard_map/pallas_call | solution.py:489
  34.0 2.3 %shard_map.71 = (f32[2,7,16,128]{3,2,1,0:T(8,128)S(1)}, f32[1024,128]{1,0:T(8,128)S(1)}, bf16[24,128,32]{2,1,0:T(8,128)(2,1)S(1)}, f32[24,128,128]{2,1,0:T(8,128)S(1)}, f32[32,128]{1,0:T(8,128)S(1)}) custom-call(s32[1]{0:T(128)} %bitcast.9.run, ...), custom_call_target="tpu_custom_call", output_to_operand_aliasing={{0}: (3, {}), {1}: (4, {}), {2}: (5, {}), {3}: (6, {}), {4}... | custom-call | flops 100000000 | bytes 4000000 | tf_op jit(solution)/shard_map/pallas_call | solution.py:489
  36.3 0.0 collective-permute-done.2.far
  36.3 0.0 collective-permute-done.3.same
  36.4 22.3 %late.1 = (f32[2,8,128]{2,1,0:T(8,128)}, f32[2,3,8,128]{3,2,1,0:T(8,128)}) custom-call(s32[2]{0:T(128)S(1)} %pad_add_fusion.info, f32[1]{0:T(128)} %bitcast.3.jump_ref, f32[136,128]{1,0:T(8,128)S(1)} %collective-permute-done.2.far, f32[136,128]{1,0:T(8,128)S(1)} %collective-permute-done.3.same, f32[2,7,16,128]{3,2,1,0:T(8,128)S(1)} %get-tuple-element.63.fields, ...), custom_call_target="tpu_custom_call" | custom-call | tf_op jit(solution)/shard_map/late/pallas_call | solution.py:553
  (4 shorter events, 0.0 us)
Async XLA Ops:
  2.2 17.1 %collective-permute-start = (f32[2,7,8,128]{3,2,1,0:T(8,128)S(1)}, f32[2,7,8,128]{3,2,1,0:T(8,128)S(1)}, u32[]{:S(2)}, u32[]{:S(2)}) collective-permute-start(f32[2,7,8,128]{3,2,1,0:T(8,128)S(1)} %pad_maximum_fusion.own), channel_id=1, source_target_pairs={{0,1},{1,2},{2,3},{3,4},{4,5},{5,6},{6,7},{7,8},{8,9},{9,10},{10,1... | collective-permute-start | bytes 172040 | tf_op jit(solution)/shard_map/ppermute | solution.py:518
  6.2 13.5 %collective-permute-start.1 = (f32[2,7,8,128]{3,2,1,0:T(8,128)S(1)}, f32[2,7,8,128]{3,2,1,0:T(8,128)S(1)}, u32[]{:S(2)}, u32[]{:S(2)}) collective-permute-start(f32[2,7,8,128]{3,2,1,0:T(8,128)S(1)} %pad_maximum_fusion.own), channel_id=1, source_target_pairs={{1,0},{2,1},{3,2},{4,3},{5,4},{6,5},{7,6},{8,7},{9,8},{10,9},{11,1... | collective-permute-start | bytes 172040 | tf_op jit(solution)/shard_map/ppermute | solution.py:520
  20.3 16.0 %collective-permute-start.2 = (f32[136,128]{1,0:T(8,128)S(1)}, f32[136,128]{1,0:T(8,128)S(1)}, u32[]{:S(2)}, u32[]{:S(2)}) collective-permute-start(f32[136,128]{1,0:T(8,128)S(1)} %get-tuple-element.36), channel_id=1, source_target_pairs={{0,480},{1,481},{2,482},{3,483},{4,484},{5,485},{6,486},{7,487},{8... | collective-permute-start | bytes 208904 | tf_op jit(solution)/shard_map/ppermute | solution.py:546
  24.8 11.5 %collective-permute-start.3 = (f32[136,128]{1,0:T(8,128)S(1)}, f32[136,128]{1,0:T(8,128)S(1)}, u32[]{:S(2)}, u32[]{:S(2)}) collective-permute-start(f32[136,128]{1,0:T(8,128)S(1)} %get-tuple-element.37), channel_id=1, source_target_pairs={{0,64},{1,65},{2,66},{3,67},{4,68},{5,69},{6,70},{7,71},{8,72},{9,... | collective-permute-start | bytes 208904 | tf_op jit(solution)/shard_map/ppermute | solution.py:548

commit v4 on v3

--- a/solution.py
+++ b/solution.py
@@ -17,6 +17,7 @@
 
 COLS, PLACES = 12, 16
 DEPTH = 32
+TERMS = 16
 NEAR = 7
 SENT = 136
 BF16, F32 = jnp.bfloat16, jnp.float32
@@ -32,7 +33,7 @@
 
 
 def place_of(column):
-    return jnp.where(column < 0, column + 10, jnp.where(column > 7, column + 2, column))
+    return column & (PLACES - 1)
 
 
 def window_kernel(info, left, own, right, far_out, same_out):
@@ -124,8 +125,11 @@
     lax.fori_loop(0, rows * count, build, 0)
 
     def turn_row(row, carry):
-        for c in range(8 * halves[0], 8 if halves[-1] == 0 else COLS):
-            cell = row * PLACES + c
+        for column in range(-2, 10):
+            if (0 if 0 <= column < 8 else 1) not in halves:
+                continue
+            c = column + 2
+            cell = row * PLACES + place_of(column)
             table = jrows[pl.ds(pl.multiple_of(cell * DEPTH, DEPTH), DEPTH), :]
             flipped = table.T.astype(BF16)
             jcols[row * COLS + c] = flipped
@@ -135,10 +139,6 @@
     lax.fori_loop(0, rows, turn_row, 0)
 
 
-def packed(cell):
-    return cell - (PLACES - COLS) * (cell // PLACES)
-
-
 def rows_of(table, cell):
     return table[pl.ds(pl.multiple_of(cell * DEPTH, DEPTH), DEPTH), :]
 
@@ -149,7 +149,6 @@
 
 
 def add_density(total, dist, m, masses, cell):
-    cell = packed(cell)
     for at in range(0, 128, 32):
         y = jnp.maximum(dist[m, at : at + 32, :], 1e-12)
         q = y * lax.rsqrt(y)
@@ -180,24 +179,22 @@
                 fields[row, f, 0:8, :] = own[row, f]
         fill_scales(scales)
         build_tables(2, (0,), fields, irows, jcols, masses, jrows)
-        jcols[8] = jnp.zeros((128, DEPTH), BF16)
-        masses[8] = jnp.zeros((128, 128), F32)
+        for at in (1, 10, COLS + 1, COLS + 10):
+            jcols[at] = jnp.zeros((128, DEPTH), BF16)
+            masses[at] = jnp.zeros((128, 128), F32)
 
         def blocks(n):
             side, column = n // 8, n % 8
-            found = []
-            for direction, row in ((1, side), (2 - 2 * side, 1 - side)):
-                for b in (-1, 0, 1):
-                    at = column + b
-                    inside = (at >= 0) & (at < 8)
-                    found.append(
-                        (row_index(direction, b), jnp.where(inside, row * PLACES + at, 8))
-                    )
+            found = [
+                (row_index(direction, b), row * COLS + column + (b + 2))
+                for direction, row in ((1, side), (2 - 2 * side, 1 - side))
+                for b in (-1, 0, 1)
+            ]
             return side * PLACES + column, found
 
         def measure(n, m):
             cell, near = blocks(n)
-            columns = jcols[packed(near[m][1])]
+            columns = jcols[near[m][1]]
             put_distances(dist, m, rows_of(irows, cell), scales[0, near[m][0]], columns)
 
         def step(n, carry):
@@ -223,8 +220,8 @@
     def _():
         for row in range(2):
             for f in range(7):
-                fields[row, f, 8:10, :] = left[row, f, 6:8, :]
-                fields[row, f, 10:12, :] = right[row, f, 0:2, :]
+                fields[row, f, 8:10, :] = right[row, f, 0:2, :]
+                fields[row, f, 14:16, :] = left[row, f, 6:8, :]
         fill_scales(scales)
         build_tables(2, (1,), fields, irows, jcols, masses, jrows)
 
@@ -234,9 +231,8 @@
             found = []
             for direction, row in ((1, side), (2 - 2 * side, 1 - side)):
                 for b in (-1, 0, 1):
-                    at = row * PLACES + place_of(outer + b)
-                    found.append((0, row_index(direction, b), at))
-                at = row * PLACES + place_of(outer)
+                    found.append((0, row_index(direction, b), row * COLS + outer + (b + 2)))
+                at = row * COLS + outer + 2
                 found.append((1, row_index(direction, 2 * far - 1), at))
             cells = [side * PLACES + place_of(column) for column in (outer, inner)]
             return cells, found
@@ -245,7 +241,7 @@
             cells, near = blocks(n)
             which, index, at = near[m]
             table = rows_of(irows, cells[which])
-            put_distances(dist, m, table, scales[0, index], jcols[packed(at)])
+            put_distances(dist, m, table, scales[0, index], jcols[at])
 
         def step(n, carry):
             cells, near = blocks(n)
@@ -278,21 +274,21 @@
             if piece is far and f == 3:
                 value = value + jump
             ghosts[side, f, 0:8, :] = value[2:10]
-            ghosts[side, f, 8:10, :] = value[0:2]
-            ghosts[side, f, 10:12, :] = value[10:12]
+            ghosts[side, f, 8:10, :] = value[10:12]
+            ghosts[side, f, 14:16, :] = value[0:2]
         for n, f in enumerate((0, 1, 2, 6)):
             at = (NEAR + n) * COLS
             value = piece[at : at + COLS, :]
             ghosts[2 + side, f, 0:8, :] = value[2:10]
-            ghosts[2 + side, f, 8:10, :] = value[0:2]
-            ghosts[2 + side, f, 10:12, :] = value[10:12]
+            ghosts[2 + side, f, 8:10, :] = value[10:12]
+            ghosts[2 + side, f, 14:16, :] = value[0:2]
     fill_scales(scales)
     build_tables(4, (0, 1), ghosts, ghost_irows, ghost_jcols, ghost_masses, jrows)
 
     def blocks(n):
         side, column = n // 10, n % 10 - 1
         return side * PLACES + place_of(column), side, [
-            (who, row_index(direction, b), row * PLACES + place_of(column + b))
+            (who, row_index(direction, b), row * COLS + column + (b + 2))
             for who, direction, row in (
                 ("far", 2 * side, side + 2),
                 ("near", 1, side),
@@ -306,7 +302,7 @@
         cell, _, near = blocks(n)
         who, index, at = near[m]
         table = rows_of(irows if who == "mine" else ghost_irows, cell)
-        columns = (jcols if who == "own" else ghost_jcols)[packed(at)]
+        columns = (jcols if who == "own" else ghost_jcols)[at]
         put_distances(dist, m, table, scales[0, index], columns)
 
     def density_step(n, carry):
@@ -335,7 +331,7 @@
     def coefficients(source, densities, target):
         def step(n, carry):
             row, half = n // 2, n % 2
-            base = n * (8 * DEPTH)
+            base = n * (8 * TERMS)
             cells = pl.ds(pl.multiple_of(half * 8, 8), 8)
             mass = source[row, 6, cells, :]
             rho = densities[pl.ds(pl.multiple_of(n * 8, 8), 8), :]
@@ -352,9 +348,7 @@
                 terms.append(share * source[row, f, cells, :])
             terms.append(jnp.zeros((8, 128), F32))
             for t, term in enumerate(terms):
-                high, low = parts_of(term, 2)
-                target[pl.ds(base + t, 8, stride=DEPTH), :] = high
-                target[pl.ds(base + 16 + t, 8, stride=DEPTH), :] = low
+                target[pl.ds(base + t, 8, stride=TERMS), :] = term
             return carry
 
         lax.fori_loop(0, 4, step, 0)
@@ -365,7 +359,7 @@
     def force_blocks(n):
         side, column = n // 8, n % 8
         return side * PLACES + column, [
-            (ghost, row_index(direction, b), row * PLACES + place_of(column + b))
+            (ghost, row_index(direction, b), row, column + b)
             for ghost, direction, row in (
                 (True, 2 * side, side),
                 (False, 1, side),
@@ -376,17 +370,20 @@
 
     def force_measure(n, m):
         cell, near = force_blocks(n)
-        ghost, index, at = near[m]
-        columns = (ghost_jcols if ghost else jcols)[packed(at)]
+        ghost, index, row, column = near[m]
+        columns = (ghost_jcols if ghost else jcols)[row * COLS + column + 2]
         put_distances(dist, m, rows_of(irows, cell), scales[0, index], columns)
 
     def gather_sums(n, slopes):
         _, near = force_blocks(n)
         total = jnp.zeros((DEPTH, 256), F32)
         for m in range(9):
-            ghost, index, at = near[m]
-            table = rows_of(ghost_crows if ghost else crows, at)
-            left_side = (table * scales[1, index]).astype(BF16)
+            ghost, index, row, column = near[m]
+            at = row * PLACES + place_of(column)
+            table = ghost_crows if ghost else crows
+            table = table[pl.ds(pl.multiple_of(at * TERMS, TERMS), TERMS), :]
+            left_side = jnp.concatenate(parts_of(table * scales[1, index, 0:TERMS, :], 2), axis=0)
+            left_side = left_side.astype(BF16)
             total = total + jnp.dot(
                 jnp.concatenate([left_side, left_side], axis=1),
                 slopes[256 * m : 256 * (m + 1), :],
@@ -471,17 +468,18 @@
     slab = lax.axis_index(rows_axis)
     past = shear_shift[0] - half * particle_mass.shape[1]
 
-    slot = jnp.arange(particle_mass.shape[2], dtype=jnp.int32)
-    weight = jnp.where(slot < cell_counts[:, :, None], particle_mass, 0.0)
     ring = [(i, (i + 1) % blocks) for i in range(blocks)]
     fields = jnp.concatenate(
         [
             jnp.transpose(position, (0, 3, 1, 2)),
             jnp.transpose(velocity, (0, 3, 1, 2)),
-            weight[:, None],
+            particle_mass[:, None],
         ],
         axis=1,
     )
+    field = lax.broadcasted_iota(jnp.int32, fields.shape, 1)
+    slot = lax.broadcasted_iota(jnp.int32, fields.shape, 3)
+    fields = jnp.where((field < 6) | (slot < cell_counts[:, None, :, None]), fields, 0.0)
     shapes = (*TABLES, jax.ShapeDtypeStruct((2 * PLACES, 128), F32))
 
     def tables_call(kernel, run, inputs, tables, blocks):
@@ -505,15 +503,12 @@
 
     block = lax.axis_index(columns_axis)
     edge = (slab == 0) | (slab == slabs - 1)
-    own_now = [block <= 1, (block > 1) & ~(edge & (block >= half)), edge & (block >= half)]
-    soon = edge & (block > 1) & (block < half)
-    beside_now = [soon, ~edge, edge & ~soon]
+    corner = (block == 0) & (slab == 0)
+    ahead, late = (block == 0) & ~corner, edge & (block >= half) | corner
+    own_now = [ahead, ~(ahead | late), late]
 
     def own_work(which, tables):
         return tables_call(own_kernel, own_now[which], (fields,), tables, 6)
-
-    def beside_work(which, tables):
-        return tables_call(beside_kernel, beside_now[which], (left, right), tables, 8)
 
     left = lax.ppermute(fields, columns_axis, ring)
     tables = own_work(0, ())
@@ -542,12 +537,10 @@
             if other < 0 or other >= slabs:
                 other, to = other % slabs, (b + half) % blocks
             far_pairs.append((me, other * blocks + to))
-    tables = beside_work(0, tables)
     far = lax.ppermute(far, axes, far_pairs)
-    tables = beside_work(1, tables)
+    tables = own_work(2, tables)
+    tables = tables_call(beside_kernel, block >= 0, (left, right), tables, 8)
     same = lax.ppermute(same, axes, same_pairs)
-    tables = own_work(2, tables)
-    tables = beside_work(2, tables)
 
     jump = jnp.where(slab == slabs - 1, SHEAR_JUMP, jnp.where(slab == 0, -SHEAR_JUMP, 0.0))
     density, accel = pl.pallas_call(
@@ -564,8 +557,8 @@
             pltpu.VMEM((2, 9, DEPTH, 128), F32),
             pltpu.VMEM((2 * PLACES, 128), F32),
             pltpu.VMEM((2 * PLACES, 128), F32),
-            pltpu.VMEM((2 * PLACES * DEPTH, 128), F32),
-            pltpu.VMEM((2 * PLACES * DEPTH, 128), F32),
+            pltpu.VMEM((2 * PLACES * TERMS, 128), F32),
+            pltpu.VMEM((2 * PLACES * TERMS, 128), F32),
             pltpu.VMEM((12, 128, 128), F32),
             pltpu.VMEM((2, 16 * 16, 128), F32),
             pltpu.VMEM((9 * 256, 256), BF16),

time: 58.9 us -> 56.9 us (0.966)
  Pallas kernels: 30.5 us -> 29.2 us
  other arithmetic: 1.61 us -> 0.94 us
    pallas_call x1, Pallas kernels: 22.3 us -> 21.1 us  [local(): pl.pallas_call(late_kernel, out_shape=(jax.ShapeDtypeStruct((2, 8, 128),...]
    select_n x0 -> x1, other arithmetic: none -> 0.85 us  [local(): jnp.where((field < 6) | (slot < cell_counts[:, None, :, None]), fields, 0.0)]
    broadcast_in_dim x1 -> x0, other arithmetic: 0.77 us -> none  [local(): weight[:, None]]
    concatenate x1 -> x0, other arithmetic: 0.76 us -> none  [local(): jnp.concatenate([jnp.transpose(position, (0, 3, 1, 2)), jnp.transpose(vel...]
    pallas_call x6 -> x4, Pallas kernels: 7.7 us -> 7.57 us  [tables_call(): pl.pallas_call(kernel, out_shape=shapes, in_specs=[SMEM] + [VMEM] * (len(...]
where the time goes in v4:
time: 56.9 us; the launch traced here: 56.6 us
  Pallas kernels  29.2 us (51%)
  starting transfers between devices  24.6 us (43%)
  between operations  1.42 us (2%)
  other arithmetic  0.94 us (2%)
    pallas_call x1, Pallas kernels, local(): pl.pallas_call(late_kernel, out_shape=(jax.ShapeDtypeStruct((2, 8, 128),...  21.1 us
    ppermute x1, starting transfers between devices, local(): right = lax.ppermute(fields, columns_axis, [(j, i) for i, j in ring])  12.3 us
    pallas_call x4, Pallas kernels, tables_call(): pl.pallas_call(kernel, out_shape=shapes, in_specs=[SMEM] + [VMEM] * (len(...  7.57 us
    ppermute x1, starting transfers between devices, local(): far = lax.ppermute(far, axes, far_pairs)  4.53 us
    ppermute x1, starting transfers between devices, local(): left = lax.ppermute(fields, columns_axis, ring)  4.02 us
    ppermute x1, starting transfers between devices, local(): same = lax.ppermute(same, axes, same_pairs)  3.71 us
  transfers between devices with their start and end apart: 4, of which 1 were waited for; matrix products, arithmetic and copies ran while one was open for 0% of the time, Pallas kernels for 13%

profile of v4, /device:TPU:1, one launch (start us, length us, event | category | flops | bytes accessed | tf_op | source)
XLA Modules:
  0.0 56.6 jit_solution(8758460234262427156)
XLA Ops:
  0.6 0.9 %maximum_select_fusion.own = f32[2,7,8,128]{3,2,1,0:T(8,128)S(1)} fusion(f32[2,1,8,128]{3,2,1,0:T(8,128)} %bitcast.14, f32[2,3,8,128]{3,2,1,0:T(8,128)} %bitcast.12, f32[2,3,8,128]{3,2,1,0:T(8,128)} %bitcast.13, s32[2,8]{1,0:T(2,128)} %param.8, pred[7]{0:T(512)(128)(4,1)S(1)} %iota_compare_fusion.1), kind=kLoop, calls=%fused_computation | loop fusion | flops 71680 | bytes 114759 | tf_op jit(solution)/shard_map/jit(_where)/select_n | solution.py:482
  1.5 4.0 %collective-permute-start = (f32[2,7,8,128]{3,2,1,0:T(8,128)S(1)}, f32[2,7,8,128]{3,2,1,0:T(8,128)S(1)}, u32[]{:S(2)}, u32[]{:S(2)}) collective-permute-start(f32[2,7,8,128]{3,2,1,0:T(8,128)S(1)} %maximum_select_fusion.own), channel_id=1, source_target_pairs={{0,1},{1,2},{2,3},{3,4},{4,5},{5,6},{6,7},{7,8},{8,9},{9,10},{10,1... | collective-permute-start | bytes 172040 | tf_op jit(solution)/shard_map/ppermute | solution.py:513
  5.5 12.3 %collective-permute-start.1 = (f32[2,7,8,128]{3,2,1,0:T(8,128)S(1)}, f32[2,7,8,128]{3,2,1,0:T(8,128)S(1)}, u32[]{:S(2)}, u32[]{:S(2)}) collective-permute-start(f32[2,7,8,128]{3,2,1,0:T(8,128)S(1)} %maximum_select_fusion.own), channel_id=1, source_target_pairs={{1,0},{2,1},{3,2},{4,3},{5,4},{6,5},{7,6},{8,7},{9,8},{10,9},{11,1... | collective-permute-start | bytes 172040 | tf_op jit(solution)/shard_map/ppermute | solution.py:515
  18.5 0.1 pad_add_fusion.info
  18.6 0.0 collective-permute-done.left
  18.6 0.5 collective-permute-done.1.right
  19.1 0.6 %window.1 = (f32[136,128]{1,0:T(8,128)S(1)}, f32[136,128]{1,0:T(8,128)S(1)}) custom-call(s32[2]{0:T(128)S(1)} %pad_add_fusion.info, f32[2,7,8,128]{3,2,1,0:T(8,128)S(1)} %collective-permute-done.left, f32[2,7,8,128]{3,2,1,0:T(8,128)S(1)} %maximum_select_fusion.own, f32[2,7,8,128]{3,2,1,0:T(8,128)S(1)} %collective-permute-done.1.right), custom_call_target="tpu_custom_call" | custom-call | tf_op jit(solution)/shard_map/window/pallas_call | solution.py:522
  19.6 4.5 %collective-permute-start.2 = (f32[136,128]{1,0:T(8,128)S(1)}, f32[136,128]{1,0:T(8,128)S(1)}, u32[]{:S(2)}, u32[]{:S(2)}) collective-permute-start(f32[136,128]{1,0:T(8,128)S(1)} %get-tuple-element.26), channel_id=1, source_target_pairs={{0,480},{1,481},{2,482},{3,483},{4,484},{5,485},{6,486},{7,487},{8... | collective-permute-start | bytes 208904 | tf_op jit(solution)/shard_map/ppermute | solution.py:540
  24.2 3.7 %collective-permute-start.3 = (f32[136,128]{1,0:T(8,128)S(1)}, f32[136,128]{1,0:T(8,128)S(1)}, u32[]{:S(2)}, u32[]{:S(2)}) collective-permute-start(f32[136,128]{1,0:T(8,128)S(1)} %get-tuple-element.27), channel_id=1, source_target_pairs={{0,64},{1,65},{2,66},{3,67},{4,68},{5,69},{6,70},{7,71},{8,72},{9,... | collective-permute-start | bytes 208904 | tf_op jit(solution)/shard_map/ppermute | solution.py:543
  27.9 5.3 %shard_map.68 = (f32[2,7,16,128]{3,2,1,0:T(8,128)S(1)}, f32[1024,128]{1,0:T(8,128)S(1)}, bf16[24,128,32]{2,1,0:T(8,128)(2,1)S(1)}, f32[24,128,128]{2,1,0:T(8,128)S(1)}, f32[32,128]{1,0:T(8,128)S(1)}) custom-call(s32[1]{0:T(128)} %bitcast.10.run, f32[2,7,8,128]{3,2,1,0:T(8,128)S(1)} %maximum_select_fusion.own), custom_call_target="tpu_custom_call" | custom-call | flops 100000000 | bytes 4000000 | tf_op jit(solution)/shard_map/pallas_call | solution.py:487
  33.2 2.3 %shard_map.71 = (f32[2,7,16,128]{3,2,1,0:T(8,128)S(1)}, f32[1024,128]{1,0:T(8,128)S(1)}, bf16[24,128,32]{2,1,0:T(8,128)(2,1)S(1)}, f32[24,128,128]{2,1,0:T(8,128)S(1)}, f32[32,128]{1,0:T(8,128)S(1)}) custom-call(s32[1]{0:T(128)} %bitcast.7.run, ...), custom_call_target="tpu_custom_call", output_to_operand_aliasing={{0}: (3, {}), {1}: (4, {}), {2}: (5, {}), {3}: (6, {}), {4}... | custom-call | flops 100000000 | bytes 4000000 | tf_op jit(solution)/shard_map/pallas_call | solution.py:487
  35.5 0.0 collective-permute-done.2.far
  35.5 0.0 collective-permute-done.3.same
  35.5 21.1 %late.1 = (f32[2,8,128]{2,1,0:T(8,128)}, f32[2,3,8,128]{3,2,1,0:T(8,128)}) custom-call(s32[2]{0:T(128)S(1)} %pad_add_fusion.info, f32[1]{0:T(128)} %bitcast.3.jump_ref, f32[136,128]{1,0:T(8,128)S(1)} %collective-permute-done.2.far, f32[136,128]{1,0:T(8,128)S(1)} %collective-permute-done.3.same, f32[2,7,16,128]{3,2,1,0:T(8,128)S(1)} %get-tuple-element.43.fields, ...), custom_call_target="tpu_custom_call" | custom-call | tf_op jit(solution)/shard_map/late/pallas_call | solution.py:546
  (3 shorter events, 0.0 us)
Async XLA Ops:
  1.5 17.1 %collective-permute-start = (f32[2,7,8,128]{3,2,1,0:T(8,128)S(1)}, f32[2,7,8,128]{3,2,1,0:T(8,128)S(1)}, u32[]{:S(2)}, u32[]{:S(2)}) collective-permute-start(f32[2,7,8,128]{3,2,1,0:T(8,128)S(1)} %maximum_select_fusion.own), channel_id=1, source_target_pairs={{0,1},{1,2},{2,3},{3,4},{4,5},{5,6},{6,7},{7,8},{8,9},{9,10},{10,1... | collective-permute-start | bytes 172040 | tf_op jit(solution)/shard_map/ppermute | solution.py:513
  5.5 13.5 %collective-permute-start.1 = (f32[2,7,8,128]{3,2,1,0:T(8,128)S(1)}, f32[2,7,8,128]{3,2,1,0:T(8,128)S(1)}, u32[]{:S(2)}, u32[]{:S(2)}) collective-permute-start(f32[2,7,8,128]{3,2,1,0:T(8,128)S(1)} %maximum_select_fusion.own), channel_id=1, source_target_pairs={{1,0},{2,1},{3,2},{4,3},{5,4},{6,5},{7,6},{8,7},{9,8},{10,9},{11,1... | collective-permute-start | bytes 172040 | tf_op jit(solution)/shard_map/ppermute | solution.py:515
  19.6 15.9 %collective-permute-start.2 = (f32[136,128]{1,0:T(8,128)S(1)}, f32[136,128]{1,0:T(8,128)S(1)}, u32[]{:S(2)}, u32[]{:S(2)}) collective-permute-start(f32[136,128]{1,0:T(8,128)S(1)} %get-tuple-element.26), channel_id=1, source_target_pairs={{0,480},{1,481},{2,482},{3,483},{4,484},{5,485},{6,486},{7,487},{8... | collective-permute-start | bytes 208904 | tf_op jit(solution)/shard_map/ppermute | solution.py:540
  24.2 11.4 %collective-permute-start.3 = (f32[136,128]{1,0:T(8,128)S(1)}, f32[136,128]{1,0:T(8,128)S(1)}, u32[]{:S(2)}, u32[]{:S(2)}) collective-permute-start(f32[136,128]{1,0:T(8,128)S(1)} %get-tuple-element.27), channel_id=1, source_target_pairs={{0,64},{1,65},{2,66},{3,67},{4,68},{5,69},{6,70},{7,71},{8,72},{9,... | collective-permute-start | bytes 208904 | tf_op jit(solution)/shard_map/ppermute | solution.py:543

commit v5 on v4

--- a/solution.py
+++ b/solution.py
@@ -124,9 +124,10 @@
 
     lax.fori_loop(0, rows * count, build, 0)
 
-    def turn_row(row, carry):
-        for column in range(-2, 10):
-            if (0 if 0 <= column < 8 else 1) not in halves:
+    def turn_rows(pair, carry):
+        for n in range(48):
+            row, column = 2 * pair + n % 2, n // 2 - 2
+            if column > 9 or (0 if 0 <= column < 8 else 1) not in halves:
                 continue
             c = column + 2
             cell = row * PLACES + place_of(column)
@@ -136,7 +137,7 @@
             masses[row * COLS + c] = jnp.dot(flipped, pick_mass, preferred_element_type=F32)
         return carry
 
-    lax.fori_loop(0, rows, turn_row, 0)
+    lax.fori_loop(0, rows // 2, turn_rows, 0)
 
 
 def rows_of(table, cell):
@@ -504,11 +505,15 @@
     block = lax.axis_index(columns_axis)
     edge = (slab == 0) | (slab == slabs - 1)
     corner = (block == 0) & (slab == 0)
-    ahead, late = (block == 0) & ~corner, edge & (block >= half) | corner
-    own_now = [ahead, ~(ahead | late), late]
+    ahead, late = (block == 0) & ~corner, edge & (block >= half)
+    own_now = [ahead, ~(ahead | late | corner), late, corner]
+    beside_now = [~corner, corner]
 
     def own_work(which, tables):
         return tables_call(own_kernel, own_now[which], (fields,), tables, 6)
+
+    def beside_work(which, tables):
+        return tables_call(beside_kernel, beside_now[which], (left, right), tables, 8)
 
     left = lax.ppermute(fields, columns_axis, ring)
     tables = own_work(0, ())
@@ -539,8 +544,10 @@
             far_pairs.append((me, other * blocks + to))
     far = lax.ppermute(far, axes, far_pairs)
     tables = own_work(2, tables)
-    tables = tables_call(beside_kernel, block >= 0, (left, right), tables, 8)
+    tables = beside_work(0, tables)
     same = lax.ppermute(same, axes, same_pairs)
+    tables = own_work(3, tables)
+    tables = beside_work(1, tables)
 
     jump = jnp.where(slab == slabs - 1, SHEAR_JUMP, jnp.where(slab == 0, -SHEAR_JUMP, 0.0))
     density, accel = pl.pallas_call(

time: 56.9 us -> 55.8 us (0.981)
  Pallas kernels: 29.2 us -> 28.1 us
    pallas_call x4 -> x6, Pallas kernels: 7.57 us -> 6.91 us  [tables_call(): pl.pallas_call(kernel, out_shape=shapes, in_specs=[SMEM] + [VMEM] * (len(...]
  transfers between devices with their start and end apart: 4 -> 4, of which waited for: 1 -> 1; matrix products, arithmetic and copies ran while one was open for 0% -> 0% of each run, Pallas kernels for 13% -> 12%
where the time goes in v5:
time: 55.8 us; the launch traced here: 55.5 us
  Pallas kernels  28.1 us (50%)
  starting transfers between devices  24.6 us (44%)
  between operations  1.44 us (3%)
  other arithmetic  0.94 us (2%)
    pallas_call x1, Pallas kernels, local(): pl.pallas_call(late_kernel, out_shape=(jax.ShapeDtypeStruct((2, 8, 128),...  20.6 us
    ppermute x1, starting transfers between devices, local(): right = lax.ppermute(fields, columns_axis, [(j, i) for i, j in ring])  12.3 us
    pallas_call x6, Pallas kernels, tables_call(): pl.pallas_call(kernel, out_shape=shapes, in_specs=[SMEM] + [VMEM] * (len(...  6.91 us
    ppermute x1, starting transfers between devices, local(): far = lax.ppermute(far, axes, far_pairs)  4.53 us
    ppermute x1, starting transfers between devices, local(): left = lax.ppermute(fields, columns_axis, ring)  4.02 us
    ppermute x1, starting transfers between devices, local(): same = lax.ppermute(same, axes, same_pairs)  3.71 us
  transfers between devices with their start and end apart: 4, of which 1 were waited for; matrix products, arithmetic and copies ran while one was open for 0% of the time, Pallas kernels for 12%

profile of v5, /device:TPU:1, one launch (start us, length us, event | category | flops | bytes accessed | tf_op | source)
XLA Modules:
  0.0 55.5 jit_solution(5481239043684251407)
XLA Ops:
  0.6 0.9 %maximum_select_fusion.own = f32[2,7,8,128]{3,2,1,0:T(8,128)S(1)} fusion(f32[2,1,8,128]{3,2,1,0:T(8,128)} %bitcast.15, f32[2,3,8,128]{3,2,1,0:T(8,128)} %bitcast.13, f32[2,3,8,128]{3,2,1,0:T(8,128)} %bitcast.14, s32[2,8]{1,0:T(2,128)} %param.8, pred[7]{0:T(512)(128)(4,1)S(1)} %iota_compare_fusion.1), kind=kLoop, calls=%fused_computation | loop fusion | flops 71680 | bytes 114759 | tf_op jit(solution)/shard_map/jit(_where)/select_n | solution.py:483
  1.5 4.0 %collective-permute-start = (f32[2,7,8,128]{3,2,1,0:T(8,128)S(1)}, f32[2,7,8,128]{3,2,1,0:T(8,128)S(1)}, u32[]{:S(2)}, u32[]{:S(2)}) collective-permute-start(f32[2,7,8,128]{3,2,1,0:T(8,128)S(1)} %maximum_select_fusion.own), channel_id=1, source_target_pairs={{0,1},{1,2},{2,3},{3,4},{4,5},{5,6},{6,7},{7,8},{8,9},{9,10},{10,1... | collective-permute-start | bytes 172040 | tf_op jit(solution)/shard_map/ppermute | solution.py:518
  5.5 12.3 %collective-permute-start.1 = (f32[2,7,8,128]{3,2,1,0:T(8,128)S(1)}, f32[2,7,8,128]{3,2,1,0:T(8,128)S(1)}, u32[]{:S(2)}, u32[]{:S(2)}) collective-permute-start(f32[2,7,8,128]{3,2,1,0:T(8,128)S(1)} %maximum_select_fusion.own), channel_id=1, source_target_pairs={{1,0},{2,1},{3,2},{4,3},{5,4},{6,5},{7,6},{8,7},{9,8},{10,9},{11,1... | collective-permute-start | bytes 172040 | tf_op jit(solution)/shard_map/ppermute | solution.py:520
  18.5 0.1 pad_add_fusion.info
  18.6 0.0 collective-permute-done.left
  18.6 0.5 collective-permute-done.1.right
  19.1 0.6 %window.1 = (f32[136,128]{1,0:T(8,128)S(1)}, f32[136,128]{1,0:T(8,128)S(1)}) custom-call(s32[2]{0:T(128)S(1)} %pad_add_fusion.info, f32[2,7,8,128]{3,2,1,0:T(8,128)S(1)} %collective-permute-done.left, f32[2,7,8,128]{3,2,1,0:T(8,128)S(1)} %maximum_select_fusion.own, f32[2,7,8,128]{3,2,1,0:T(8,128)S(1)} %collective-permute-done.1.right), custom_call_target="tpu_custom_call" | custom-call | tf_op jit(solution)/shard_map/window/pallas_call | solution.py:527
  19.6 4.5 %collective-permute-start.2 = (f32[136,128]{1,0:T(8,128)S(1)}, f32[136,128]{1,0:T(8,128)S(1)}, u32[]{:S(2)}, u32[]{:S(2)}) collective-permute-start(f32[136,128]{1,0:T(8,128)S(1)} %get-tuple-element.36), channel_id=1, source_target_pairs={{0,480},{1,481},{2,482},{3,483},{4,484},{5,485},{6,486},{7,487},{8... | collective-permute-start | bytes 208904 | tf_op jit(solution)/shard_map/ppermute | solution.py:545
  24.2 3.7 %collective-permute-start.3 = (f32[136,128]{1,0:T(8,128)S(1)}, f32[136,128]{1,0:T(8,128)S(1)}, u32[]{:S(2)}, u32[]{:S(2)}) collective-permute-start(f32[136,128]{1,0:T(8,128)S(1)} %get-tuple-element.37), channel_id=1, source_target_pairs={{0,64},{1,65},{2,66},{3,67},{4,68},{5,69},{6,70},{7,71},{8,72},{9,... | collective-permute-start | bytes 208904 | tf_op jit(solution)/shard_map/ppermute | solution.py:548
  27.9 4.9 %shard_map.68 = (f32[2,7,16,128]{3,2,1,0:T(8,128)S(1)}, f32[1024,128]{1,0:T(8,128)S(1)}, bf16[24,128,32]{2,1,0:T(8,128)(2,1)S(1)}, f32[24,128,128]{2,1,0:T(8,128)S(1)}, f32[32,128]{1,0:T(8,128)S(1)}) custom-call(s32[1]{0:T(128)} %bitcast.11.run, f32[2,7,8,128]{3,2,1,0:T(8,128)S(1)} %maximum_select_fusion.own), custom_call_target="tpu_custom_call" | custom-call | flops 100000000 | bytes 4000000 | tf_op jit(solution)/shard_map/pallas_call | solution.py:488
  32.9 2.0 %shard_map.71 = (f32[2,7,16,128]{3,2,1,0:T(8,128)S(1)}, f32[1024,128]{1,0:T(8,128)S(1)}, bf16[24,128,32]{2,1,0:T(8,128)(2,1)S(1)}, f32[24,128,128]{2,1,0:T(8,128)S(1)}, f32[32,128]{1,0:T(8,128)S(1)}) custom-call(s32[1]{0:T(128)} %bitcast.8.run, ...), custom_call_target="tpu_custom_call", output_to_operand_aliasing={{0}: (3, {}), {1}: (4, {}), {2}: (5, {}), {3}: (6, {}), {4}... | custom-call | flops 100000000 | bytes 4000000 | tf_op jit(solution)/shard_map/pallas_call | solution.py:488
  34.9 0.0 collective-permute-done.2.far
  34.9 0.0 collective-permute-done.3.same
  34.9 20.6 %late.1 = (f32[2,8,128]{2,1,0:T(8,128)}, f32[2,3,8,128]{3,2,1,0:T(8,128)}) custom-call(s32[2]{0:T(128)S(1)} %pad_add_fusion.info, f32[1]{0:T(128)} %bitcast.3.jump_ref, f32[136,128]{1,0:T(8,128)S(1)} %collective-permute-done.2.far, f32[136,128]{1,0:T(8,128)S(1)} %collective-permute-done.3.same, f32[2,7,16,128]{3,2,1,0:T(8,128)S(1)} %get-tuple-element.63.fields, ...), custom_call_target="tpu_custom_call" | custom-call | tf_op jit(solution)/shard_map/late/pallas_call | solution.py:553
  (5 shorter events, 0.1 us)
Async XLA Ops:
  1.5 17.1 %collective-permute-start = (f32[2,7,8,128]{3,2,1,0:T(8,128)S(1)}, f32[2,7,8,128]{3,2,1,0:T(8,128)S(1)}, u32[]{:S(2)}, u32[]{:S(2)}) collective-permute-start(f32[2,7,8,128]{3,2,1,0:T(8,128)S(1)} %maximum_select_fusion.own), channel_id=1, source_target_pairs={{0,1},{1,2},{2,3},{3,4},{4,5},{5,6},{6,7},{7,8},{8,9},{9,10},{10,1... | collective-permute-start | bytes 172040 | tf_op jit(solution)/shard_map/ppermute | solution.py:518
  5.5 13.5 %collective-permute-start.1 = (f32[2,7,8,128]{3,2,1,0:T(8,128)S(1)}, f32[2,7,8,128]{3,2,1,0:T(8,128)S(1)}, u32[]{:S(2)}, u32[]{:S(2)}) collective-permute-start(f32[2,7,8,128]{3,2,1,0:T(8,128)S(1)} %maximum_select_fusion.own), channel_id=1, source_target_pairs={{1,0},{2,1},{3,2},{4,3},{5,4},{6,5},{7,6},{8,7},{9,8},{10,9},{11,1... | collective-permute-start | bytes 172040 | tf_op jit(solution)/shard_map/ppermute | solution.py:520
  19.6 15.2 %collective-permute-start.2 = (f32[136,128]{1,0:T(8,128)S(1)}, f32[136,128]{1,0:T(8,128)S(1)}, u32[]{:S(2)}, u32[]{:S(2)}) collective-permute-start(f32[136,128]{1,0:T(8,128)S(1)} %get-tuple-element.36), channel_id=1, source_target_pairs={{0,480},{1,481},{2,482},{3,483},{4,484},{5,485},{6,486},{7,487},{8... | collective-permute-start | bytes 208904 | tf_op jit(solution)/shard_map/ppermute | solution.py:545
  24.2 10.7 %collective-permute-start.3 = (f32[136,128]{1,0:T(8,128)S(1)}, f32[136,128]{1,0:T(8,128)S(1)}, u32[]{:S(2)}, u32[]{:S(2)}) collective-permute-start(f32[136,128]{1,0:T(8,128)S(1)} %get-tuple-element.37), channel_id=1, source_target_pairs={{0,64},{1,65},{2,66},{3,67},{4,68},{5,69},{6,70},{7,71},{8,72},{9,... | collective-permute-start | bytes 208904 | tf_op jit(solution)/shard_map/ppermute | solution.py:548

commit v6 on v5

--- a/solution.py
+++ b/solution.py
@@ -1,3 +1,4 @@
+import functools
 import math
 
 import jax
@@ -79,7 +80,8 @@
             scales[1, n] = scale
 
 
-def build_tables(rows, halves, fields, irows, jcols, masses, jrows):
+def build_tables(rows, halves, fields, irows, jcols, masses, jrows, irows_of=None):
+    irows_of = rows if irows_of is None else irows_of
     k = lax.broadcasted_iota(jnp.int32, (DEPTH, 128), 0)
     ones_j = jnp.where(((k >= 15) & (k < 20)) | (k == 22) | (k == 23) | (k == 26), 1.0, 0.0)
     ones_i = jnp.where((k >= 12) & (k < 15), 1.0, 0.0)
@@ -88,16 +90,19 @@
 
     count = len(halves)
 
-    def build(n, carry):
+    def build(n, carry, with_irows=True):
         row, half = n // count, n % count + halves[0]
         step = row * 2 + half
         base = pl.multiple_of(step * (8 * DEPTH), 8 * DEPTH)
         cells = pl.ds(pl.multiple_of(half * 8, 8), 8)
         for c in range(8):
             jrows[pl.ds(base + c * DEPTH, DEPTH), :] = ones_j
-            irows[pl.ds(base + c * DEPTH, DEPTH), :] = ones_i
+            if with_irows:
+                irows[pl.ds(base + c * DEPTH, DEPTH), :] = ones_i
 
         def put(table, k, value):
+            if table is irows and not with_irows:
+                return
             table[pl.ds(base + k, 8, stride=DEPTH), :] = value
 
         norm = jnp.zeros((8, 128), F32)
@@ -122,7 +127,10 @@
             put(jrows, 27 + k, part)
         return carry
 
-    lax.fori_loop(0, rows * count, build, 0)
+    lax.fori_loop(0, irows_of * count, build, 0)
+    if irows_of < rows:
+        rest = functools.partial(build, with_irows=False)
+        lax.fori_loop(irows_of * count, rows * count, rest, 0)
 
     def turn_rows(pair, carry):
         for n in range(48):
@@ -211,7 +219,7 @@
         rhos[...] = jnp.zeros_like(rhos)
         for m in range(6):
             measure(0, m)
-        lax.fori_loop(0, 16, step, 0)
+        lax.fori_loop(0, 16, step, 0, unroll=2)
 
 
 def beside_kernel(run, left, right, *refs):
@@ -284,7 +292,7 @@
             ghosts[2 + side, f, 8:10, :] = value[10:12]
             ghosts[2 + side, f, 14:16, :] = value[0:2]
     fill_scales(scales)
-    build_tables(4, (0, 1), ghosts, ghost_irows, ghost_jcols, ghost_masses, jrows)
+    build_tables(4, (0, 1), ghosts, ghost_irows, ghost_jcols, ghost_masses, jrows, 2)
 
     def blocks(n):
         side, column = n // 10, n % 10 - 1
@@ -327,7 +335,7 @@
     ghost_rhos[...] = jnp.zeros_like(ghost_rhos)
     for m in range(12):
         measure(0, m)
-    lax.fori_loop(0, 20, density_step, 0)
+    lax.fori_loop(0, 20, density_step, 0, unroll=2)
 
     def coefficients(source, densities, target):
         def step(n, carry):
@@ -559,7 +567,9 @@
         in_specs=[SMEM, SMEM] + [VMEM] * 7,
         out_specs=(VMEM, VMEM),
         scratch_shapes=[
-            *scratch_of(TABLES, 4),
+            *scratch_of(TABLES[:1], 4),
+            *scratch_of(TABLES[1:2], 2),
+            *scratch_of(TABLES[2:], 4),
             pltpu.VMEM((4 * PLACES * DEPTH, 128), F32),
             pltpu.VMEM((2, 9, DEPTH, 128), F32),
             pltpu.VMEM((2 * PLACES, 128), F32),

time: 55.8 us -> 55 us (0.986)
  Pallas kernels: 28.1 us -> 27.3 us
where the time goes in v6:
time: 55 us; the launch traced here: 54.7 us
  Pallas kernels  27.3 us (50%)
  starting transfers between devices  24.6 us (45%)
  between operations  1.44 us (3%)
  other arithmetic  0.94 us (2%)
    pallas_call x1, Pallas kernels, local(): pl.pallas_call(late_kernel, out_shape=(jax.ShapeDtypeStruct((2, 8, 128),...  20.3 us
    ppermute x1, starting transfers between devices, local(): right = lax.ppermute(fields, columns_axis, [(j, i) for i, j in ring])  12.3 us
    pallas_call x6, Pallas kernels, tables_call(): pl.pallas_call(kernel, out_shape=shapes, in_specs=[SMEM] + [VMEM] * (len(...  6.43 us
    ppermute x1, starting transfers between devices, local(): far = lax.ppermute(far, axes, far_pairs)  4.53 us
    ppermute x1, starting transfers between devices, local(): left = lax.ppermute(fields, columns_axis, ring)  4.02 us
    ppermute x1, starting transfers between devices, local(): same = lax.ppermute(same, axes, same_pairs)  3.71 us
  transfers between devices with their start and end apart: 4, of which 1 were waited for; matrix products, arithmetic and copies ran while one was open for 0% of the time, Pallas kernels for 12%

profile of v6, /device:TPU:1, one launch (start us, length us, event | category | flops | bytes accessed | tf_op | source)
XLA Modules:
  0.0 54.7 jit_solution(12507315160337314373)
XLA Ops:
  0.6 0.9 %maximum_select_fusion.own = f32[2,7,8,128]{3,2,1,0:T(8,128)S(1)} fusion(f32[2,1,8,128]{3,2,1,0:T(8,128)} %bitcast.15, f32[2,3,8,128]{3,2,1,0:T(8,128)} %bitcast.13, f32[2,3,8,128]{3,2,1,0:T(8,128)} %bitcast.14, s32[2,8]{1,0:T(2,128)} %param.8, pred[7]{0:T(512)(128)(4,1)S(1)} %iota_compare_fusion.1), kind=kLoop, calls=%fused_computation | loop fusion | flops 71680 | bytes 114759 | tf_op jit(solution)/shard_map/jit(_where)/select_n | solution.py:491
  1.5 4.0 %collective-permute-start = (f32[2,7,8,128]{3,2,1,0:T(8,128)S(1)}, f32[2,7,8,128]{3,2,1,0:T(8,128)S(1)}, u32[]{:S(2)}, u32[]{:S(2)}) collective-permute-start(f32[2,7,8,128]{3,2,1,0:T(8,128)S(1)} %maximum_select_fusion.own), channel_id=1, source_target_pairs={{0,1},{1,2},{2,3},{3,4},{4,5},{5,6},{6,7},{7,8},{8,9},{9,10},{10,1... | collective-permute-start | bytes 172040 | tf_op jit(solution)/shard_map/ppermute | solution.py:526
  5.5 12.3 %collective-permute-start.1 = (f32[2,7,8,128]{3,2,1,0:T(8,128)S(1)}, f32[2,7,8,128]{3,2,1,0:T(8,128)S(1)}, u32[]{:S(2)}, u32[]{:S(2)}) collective-permute-start(f32[2,7,8,128]{3,2,1,0:T(8,128)S(1)} %maximum_select_fusion.own), channel_id=1, source_target_pairs={{1,0},{2,1},{3,2},{4,3},{5,4},{6,5},{7,6},{8,7},{9,8},{10,9},{11,1... | collective-permute-start | bytes 172040 | tf_op jit(solution)/shard_map/ppermute | solution.py:528
  18.5 0.1 pad_add_fusion.info
  18.6 0.0 collective-permute-done.left
  18.6 0.5 collective-permute-done.1.right
  19.1 0.6 %window.1 = (f32[136,128]{1,0:T(8,128)S(1)}, f32[136,128]{1,0:T(8,128)S(1)}) custom-call(s32[2]{0:T(128)S(1)} %pad_add_fusion.info, f32[2,7,8,128]{3,2,1,0:T(8,128)S(1)} %collective-permute-done.left, f32[2,7,8,128]{3,2,1,0:T(8,128)S(1)} %maximum_select_fusion.own, f32[2,7,8,128]{3,2,1,0:T(8,128)S(1)} %collective-permute-done.1.right), custom_call_target="tpu_custom_call" | custom-call | tf_op jit(solution)/shard_map/window/pallas_call | solution.py:535
  19.6 4.5 %collective-permute-start.2 = (f32[136,128]{1,0:T(8,128)S(1)}, f32[136,128]{1,0:T(8,128)S(1)}, u32[]{:S(2)}, u32[]{:S(2)}) collective-permute-start(f32[136,128]{1,0:T(8,128)S(1)} %get-tuple-element.36), channel_id=1, source_target_pairs={{0,480},{1,481},{2,482},{3,483},{4,484},{5,485},{6,486},{7,487},{8... | collective-permute-start | bytes 208904 | tf_op jit(solution)/shard_map/ppermute | solution.py:553
  24.2 3.7 %collective-permute-start.3 = (f32[136,128]{1,0:T(8,128)S(1)}, f32[136,128]{1,0:T(8,128)S(1)}, u32[]{:S(2)}, u32[]{:S(2)}) collective-permute-start(f32[136,128]{1,0:T(8,128)S(1)} %get-tuple-element.37), channel_id=1, source_target_pairs={{0,64},{1,65},{2,66},{3,67},{4,68},{5,69},{6,70},{7,71},{8,72},{9,... | collective-permute-start | bytes 208904 | tf_op jit(solution)/shard_map/ppermute | solution.py:556
  27.9 4.4 %shard_map.68 = (f32[2,7,16,128]{3,2,1,0:T(8,128)S(1)}, f32[1024,128]{1,0:T(8,128)S(1)}, bf16[24,128,32]{2,1,0:T(8,128)(2,1)S(1)}, f32[24,128,128]{2,1,0:T(8,128)S(1)}, f32[32,128]{1,0:T(8,128)S(1)}) custom-call(s32[1]{0:T(128)} %bitcast.11.run, f32[2,7,8,128]{3,2,1,0:T(8,128)S(1)} %maximum_select_fusion.own), custom_call_target="tpu_custom_call" | custom-call | flops 100000000 | bytes 4000000 | tf_op jit(solution)/shard_map/pallas_call | solution.py:496
  32.4 1.9 %shard_map.71 = (f32[2,7,16,128]{3,2,1,0:T(8,128)S(1)}, f32[1024,128]{1,0:T(8,128)S(1)}, bf16[24,128,32]{2,1,0:T(8,128)(2,1)S(1)}, f32[24,128,128]{2,1,0:T(8,128)S(1)}, f32[32,128]{1,0:T(8,128)S(1)}) custom-call(s32[1]{0:T(128)} %bitcast.8.run, ...), custom_call_target="tpu_custom_call", output_to_operand_aliasing={{0}: (3, {}), {1}: (4, {}), {2}: (5, {}), {3}: (6, {}), {4}... | custom-call | flops 100000000 | bytes 4000000 | tf_op jit(solution)/shard_map/pallas_call | solution.py:496
  34.4 0.0 collective-permute-done.2.far
  34.4 0.0 collective-permute-done.3.same
  34.4 20.3 %late.1 = (f32[2,8,128]{2,1,0:T(8,128)}, f32[2,3,8,128]{3,2,1,0:T(8,128)}) custom-call(s32[2]{0:T(128)S(1)} %pad_add_fusion.info, f32[1]{0:T(128)} %bitcast.3.jump_ref, f32[136,128]{1,0:T(8,128)S(1)} %collective-permute-done.2.far, f32[136,128]{1,0:T(8,128)S(1)} %collective-permute-done.3.same, f32[2,7,16,128]{3,2,1,0:T(8,128)S(1)} %get-tuple-element.63.fields, ...), custom_call_target="tpu_custom_call" | custom-call | tf_op jit(solution)/shard_map/late/pallas_call | solution.py:561
  (5 shorter events, 0.1 us)
Async XLA Ops:
  1.5 17.1 %collective-permute-start = (f32[2,7,8,128]{3,2,1,0:T(8,128)S(1)}, f32[2,7,8,128]{3,2,1,0:T(8,128)S(1)}, u32[]{:S(2)}, u32[]{:S(2)}) collective-permute-start(f32[2,7,8,128]{3,2,1,0:T(8,128)S(1)} %maximum_select_fusion.own), channel_id=1, source_target_pairs={{0,1},{1,2},{2,3},{3,4},{4,5},{5,6},{6,7},{7,8},{8,9},{9,10},{10,1... | collective-permute-start | bytes 172040 | tf_op jit(solution)/shard_map/ppermute | solution.py:526
  5.5 13.5 %collective-permute-start.1 = (f32[2,7,8,128]{3,2,1,0:T(8,128)S(1)}, f32[2,7,8,128]{3,2,1,0:T(8,128)S(1)}, u32[]{:S(2)}, u32[]{:S(2)}) collective-permute-start(f32[2,7,8,128]{3,2,1,0:T(8,128)S(1)} %maximum_select_fusion.own), channel_id=1, source_target_pairs={{1,0},{2,1},{3,2},{4,3},{5,4},{6,5},{7,6},{8,7},{9,8},{10,9},{11,1... | collective-permute-start | bytes 172040 | tf_op jit(solution)/shard_map/ppermute | solution.py:528
  19.6 14.8 %collective-permute-start.2 = (f32[136,128]{1,0:T(8,128)S(1)}, f32[136,128]{1,0:T(8,128)S(1)}, u32[]{:S(2)}, u32[]{:S(2)}) collective-permute-start(f32[136,128]{1,0:T(8,128)S(1)} %get-tuple-element.36), channel_id=1, source_target_pairs={{0,480},{1,481},{2,482},{3,483},{4,484},{5,485},{6,486},{7,487},{8... | collective-permute-start | bytes 208904 | tf_op jit(solution)/shard_map/ppermute | solution.py:553
  24.2 10.2 %collective-permute-start.3 = (f32[136,128]{1,0:T(8,128)S(1)}, f32[136,128]{1,0:T(8,128)S(1)}, u32[]{:S(2)}, u32[]{:S(2)}) collective-permute-start(f32[136,128]{1,0:T(8,128)S(1)} %get-tuple-element.37), channel_id=1, source_target_pairs={{0,64},{1,65},{2,66},{3,67},{4,68},{5,69},{6,70},{7,71},{8,72},{9,... | collective-permute-start | bytes 208904 | tf_op jit(solution)/shard_map/ppermute | solution.py:556

commit v7 on v6

--- a/solution.py
+++ b/solution.py
@@ -266,7 +266,7 @@
 
         for m in range(8):
             measure(0, m)
-        lax.fori_loop(0, 4, step, 0)
+        lax.fori_loop(0, 4, step, 0, unroll=2)
 
 
 def late_kernel(
@@ -335,7 +335,7 @@
     ghost_rhos[...] = jnp.zeros_like(ghost_rhos)
     for m in range(12):
         measure(0, m)
-    lax.fori_loop(0, 20, density_step, 0, unroll=2)
+    lax.fori_loop(0, 20, density_step, 0, unroll=4)
 
     def coefficients(source, densities, target):
         def step(n, carry):
@@ -360,7 +360,7 @@
                 target[pl.ds(base + t, 8, stride=TERMS), :] = term
             return carry
 
-        lax.fori_loop(0, 4, step, 0)
+        lax.fori_loop(0, 4, step, 0, unroll=2)
 
     coefficients(fields, rhos, crows)
     coefficients(ghosts, ghost_rhos, ghost_crows)

time: 55 us -> 55.2 us (level)
  transfers between devices with their start and end apart: 4 -> 4, of which waited for: 1 -> 1; matrix products, arithmetic and copies ran while one was open for 0% -> 0% of each run, Pallas kernels for 12% -> 11%
where the time goes in v7:
time: 55.2 us; the launch traced here: 54.9 us
  Pallas kernels  27.5 us (50%)
  starting transfers between devices  24.6 us (45%)
  between operations  1.44 us (3%)
  other arithmetic  0.94 us (2%)
    pallas_call x1, Pallas kernels, local(): pl.pallas_call(late_kernel, out_shape=(jax.ShapeDtypeStruct((2, 8, 128),...  20.6 us
    ppermute x1, starting transfers between devices, local(): right = lax.ppermute(fields, columns_axis, [(j, i) for i, j in ring])  12.3 us
    pallas_call x6, Pallas kernels, tables_call(): pl.pallas_call(kernel, out_shape=shapes, in_specs=[SMEM] + [VMEM] * (len(...  6.24 us
    ppermute x1, starting transfers between devices, local(): far = lax.ppermute(far, axes, far_pairs)  4.53 us
    ppermute x1, starting transfers between devices, local(): left = lax.ppermute(fields, columns_axis, ring)  4.02 us
    ppermute x1, starting transfers between devices, local(): same = lax.ppermute(same, axes, same_pairs)  3.71 us
  transfers between devices with their start and end apart: 4, of which 1 were waited for; matrix products, arithmetic and copies ran while one was open for 0% of the time, Pallas kernels for 11%

profile of v7, /device:TPU:1, one launch (start us, length us, event | category | flops | bytes accessed | tf_op | source)
XLA Modules:
  0.0 54.9 jit_solution(8156083616667059363)
XLA Ops:
  0.6 0.9 %maximum_select_fusion.own = f32[2,7,8,128]{3,2,1,0:T(8,128)S(1)} fusion(f32[2,1,8,128]{3,2,1,0:T(8,128)} %bitcast.15, f32[2,3,8,128]{3,2,1,0:T(8,128)} %bitcast.13, f32[2,3,8,128]{3,2,1,0:T(8,128)} %bitcast.14, s32[2,8]{1,0:T(2,128)} %param.8, pred[7]{0:T(512)(128)(4,1)S(1)} %iota_compare_fusion.1), kind=kLoop, calls=%fused_computation | loop fusion | flops 71680 | bytes 114759 | tf_op jit(solution)/shard_map/jit(_where)/select_n | solution.py:491
  1.5 4.0 %collective-permute-start = (f32[2,7,8,128]{3,2,1,0:T(8,128)S(1)}, f32[2,7,8,128]{3,2,1,0:T(8,128)S(1)}, u32[]{:S(2)}, u32[]{:S(2)}) collective-permute-start(f32[2,7,8,128]{3,2,1,0:T(8,128)S(1)} %maximum_select_fusion.own), channel_id=1, source_target_pairs={{0,1},{1,2},{2,3},{3,4},{4,5},{5,6},{6,7},{7,8},{8,9},{9,10},{10,1... | collective-permute-start | bytes 172040 | tf_op jit(solution)/shard_map/ppermute | solution.py:526
  5.5 12.3 %collective-permute-start.1 = (f32[2,7,8,128]{3,2,1,0:T(8,128)S(1)}, f32[2,7,8,128]{3,2,1,0:T(8,128)S(1)}, u32[]{:S(2)}, u32[]{:S(2)}) collective-permute-start(f32[2,7,8,128]{3,2,1,0:T(8,128)S(1)} %maximum_select_fusion.own), channel_id=1, source_target_pairs={{1,0},{2,1},{3,2},{4,3},{5,4},{6,5},{7,6},{8,7},{9,8},{10,9},{11,1... | collective-permute-start | bytes 172040 | tf_op jit(solution)/shard_map/ppermute | solution.py:528
  18.5 0.1 pad_add_fusion.info
  18.6 0.0 collective-permute-done.left
  18.6 0.5 collective-permute-done.1.right
  19.1 0.6 %window.1 = (f32[136,128]{1,0:T(8,128)S(1)}, f32[136,128]{1,0:T(8,128)S(1)}) custom-call(s32[2]{0:T(128)S(1)} %pad_add_fusion.info, f32[2,7,8,128]{3,2,1,0:T(8,128)S(1)} %collective-permute-done.left, f32[2,7,8,128]{3,2,1,0:T(8,128)S(1)} %maximum_select_fusion.own, f32[2,7,8,128]{3,2,1,0:T(8,128)S(1)} %collective-permute-done.1.right), custom_call_target="tpu_custom_call" | custom-call | tf_op jit(solution)/shard_map/window/pallas_call | solution.py:535
  19.6 4.5 %collective-permute-start.2 = (f32[136,128]{1,0:T(8,128)S(1)}, f32[136,128]{1,0:T(8,128)S(1)}, u32[]{:S(2)}, u32[]{:S(2)}) collective-permute-start(f32[136,128]{1,0:T(8,128)S(1)} %get-tuple-element.36), channel_id=1, source_target_pairs={{0,480},{1,481},{2,482},{3,483},{4,484},{5,485},{6,486},{7,487},{8... | collective-permute-start | bytes 208904 | tf_op jit(solution)/shard_map/ppermute | solution.py:553
  24.2 3.7 %collective-permute-start.3 = (f32[136,128]{1,0:T(8,128)S(1)}, f32[136,128]{1,0:T(8,128)S(1)}, u32[]{:S(2)}, u32[]{:S(2)}) collective-permute-start(f32[136,128]{1,0:T(8,128)S(1)} %get-tuple-element.37), channel_id=1, source_target_pairs={{0,64},{1,65},{2,66},{3,67},{4,68},{5,69},{6,70},{7,71},{8,72},{9,... | collective-permute-start | bytes 208904 | tf_op jit(solution)/shard_map/ppermute | solution.py:556
  27.9 4.4 %shard_map.68 = (f32[2,7,16,128]{3,2,1,0:T(8,128)S(1)}, f32[1024,128]{1,0:T(8,128)S(1)}, bf16[24,128,32]{2,1,0:T(8,128)(2,1)S(1)}, f32[24,128,128]{2,1,0:T(8,128)S(1)}, f32[32,128]{1,0:T(8,128)S(1)}) custom-call(s32[1]{0:T(128)} %bitcast.11.run, f32[2,7,8,128]{3,2,1,0:T(8,128)S(1)} %maximum_select_fusion.own), custom_call_target="tpu_custom_call" | custom-call | flops 100000000 | bytes 4000000 | tf_op jit(solution)/shard_map/pallas_call | solution.py:496
  32.4 1.8 %shard_map.71 = (f32[2,7,16,128]{3,2,1,0:T(8,128)S(1)}, f32[1024,128]{1,0:T(8,128)S(1)}, bf16[24,128,32]{2,1,0:T(8,128)(2,1)S(1)}, f32[24,128,128]{2,1,0:T(8,128)S(1)}, f32[32,128]{1,0:T(8,128)S(1)}) custom-call(s32[1]{0:T(128)} %bitcast.8.run, ...), custom_call_target="tpu_custom_call", output_to_operand_aliasing={{0}: (3, {}), {1}: (4, {}), {2}: (5, {}), {3}: (6, {}), {4}... | custom-call | flops 100000000 | bytes 4000000 | tf_op jit(solution)/shard_map/pallas_call | solution.py:496
  34.2 0.0 collective-permute-done.2.far
  34.2 0.0 collective-permute-done.3.same
  34.2 20.6 %late.1 = (f32[2,8,128]{2,1,0:T(8,128)}, f32[2,3,8,128]{3,2,1,0:T(8,128)}) custom-call(s32[2]{0:T(128)S(1)} %pad_add_fusion.info, f32[1]{0:T(128)} %bitcast.3.jump_ref, f32[136,128]{1,0:T(8,128)S(1)} %collective-permute-done.2.far, f32[136,128]{1,0:T(8,128)S(1)} %collective-permute-done.3.same, f32[2,7,16,128]{3,2,1,0:T(8,128)S(1)} %get-tuple-element.63.fields, ...), custom_call_target="tpu_custom_call" | custom-call | tf_op jit(solution)/shard_map/late/pallas_call | solution.py:561
  (5 shorter events, 0.1 us)
Async XLA Ops:
  1.5 17.1 %collective-permute-start = (f32[2,7,8,128]{3,2,1,0:T(8,128)S(1)}, f32[2,7,8,128]{3,2,1,0:T(8,128)S(1)}, u32[]{:S(2)}, u32[]{:S(2)}) collective-permute-start(f32[2,7,8,128]{3,2,1,0:T(8,128)S(1)} %maximum_select_fusion.own), channel_id=1, source_target_pairs={{0,1},{1,2},{2,3},{3,4},{4,5},{5,6},{6,7},{7,8},{8,9},{9,10},{10,1... | collective-permute-start | bytes 172040 | tf_op jit(solution)/shard_map/ppermute | solution.py:526
  5.5 13.5 %collective-permute-start.1 = (f32[2,7,8,128]{3,2,1,0:T(8,128)S(1)}, f32[2,7,8,128]{3,2,1,0:T(8,128)S(1)}, u32[]{:S(2)}, u32[]{:S(2)}) collective-permute-start(f32[2,7,8,128]{3,2,1,0:T(8,128)S(1)} %maximum_select_fusion.own), channel_id=1, source_target_pairs={{1,0},{2,1},{3,2},{4,3},{5,4},{6,5},{7,6},{8,7},{9,8},{10,9},{11,1... | collective-permute-start | bytes 172040 | tf_op jit(solution)/shard_map/ppermute | solution.py:528
  19.6 14.6 %collective-permute-start.2 = (f32[136,128]{1,0:T(8,128)S(1)}, f32[136,128]{1,0:T(8,128)S(1)}, u32[]{:S(2)}, u32[]{:S(2)}) collective-permute-start(f32[136,128]{1,0:T(8,128)S(1)} %get-tuple-element.36), channel_id=1, source_target_pairs={{0,480},{1,481},{2,482},{3,483},{4,484},{5,485},{6,486},{7,487},{8... | collective-permute-start | bytes 208904 | tf_op jit(solution)/shard_map/ppermute | solution.py:553
  24.2 10.1 %collective-permute-start.3 = (f32[136,128]{1,0:T(8,128)S(1)}, f32[136,128]{1,0:T(8,128)S(1)}, u32[]{:S(2)}, u32[]{:S(2)}) collective-permute-start(f32[136,128]{1,0:T(8,128)S(1)} %get-tuple-element.37), channel_id=1, source_target_pairs={{0,64},{1,65},{2,66},{3,67},{4,68},{5,69},{6,70},{7,71},{8,72},{9,... | collective-permute-start | bytes 208904 | tf_op jit(solution)/shard_map/ppermute | solution.py:556
